TPU v7x, 128 devices: a whole 4x4x4 slice. The times are simulated.
128 devices in a mesh: dp: 1, tp: 16 (over z, y), wg: 8 (over x, core).
Axes of the slice: x: 4, y: 4, z: 4, core: 2. Of those that a mesh axis runs over, the one named last changes fastest.
Arguments:
- tokens: bfloat16 [4096, 2560], P(('dp', 'wg'))
- gain_attn: float32 [2560], P('wg')
- gain_mlp: float32 [2560], P('wg')
- w_qkv: bfloat16 [2560, 3, 32, 80], P('wg', None, 'tp')
- w_rel: bfloat16 [2560, 32, 80], P('wg', 'tp')
- w_out: bfloat16 [32, 80, 2560], P('tp', None, 'wg')
- w_up: bfloat16 [2560, 10240], P('wg', 'tp')
- w_down: bfloat16 [10240, 2560], P('tp', 'wg')
- bias_u: float32 [32, 80], P('tp')
- bias_v: float32 [32, 80], P('tp')
- rel_table: bfloat16 [32, 2560], replicated
- k_cache: bfloat16 [4096, 32, 32, 80], P(('dp', 'wg'), 'tp')
- v_cache: bfloat16 [4096, 32, 32, 80], P(('dp', 'wg'), 'tp')
- positions: int32 [4096], P(('dp', 'wg'))
Outputs:
- output 1: bfloat16 [4096, 2560], P(('dp', 'wg'))
- output 2: bfloat16 [4096, 32, 80], P(('dp', 'wg'), 'tp')
- output 3: bfloat16 [4096, 32, 80], P(('dp', 'wg'), 'tp')
All inputs are finite; a program needn't handle non-finite values.
Results may differ from a plain program's by a relative error of at most 0.015003.
Values are sent between devices in bfloat16 or wider.
A program may use at most 1 GiB of HBM per device.

v0:
```python
import jax
import jax.numpy as jnp
from jax import lax
from jax.sharding import PartitionSpec as P

NORM_EPS = 1e-6


def rms_norm(row_vals, gain_vec):
    vals_f32 = row_vals.astype(jnp.float32)
    mean_sq = jnp.mean(vals_f32 * vals_f32, axis=-1, keepdims=True)
    return (vals_f32 * lax.rsqrt(mean_sq + NORM_EPS) * gain_vec).astype(jnp.bfloat16)


def cache_attention(q_u, q_v, k_new, v_new, k_cache, v_cache, positions, rel_proj):
    cache_len = k_cache.shape[2]
    score_scale = q_u.shape[-1] ** -0.5
    key_steps = jnp.arange(cache_len)
    is_self = (key_steps[None, :] == positions[:, None])[:, None, :]
    is_valid = (key_steps[None, :] <= positions[:, None])[:, None, :]
    content = jnp.einsum("bhe,bhje->bhj", q_u, k_cache, preferred_element_type=jnp.float32)
    self_score = jnp.einsum("bhe,bhe->bh", q_u, k_new, preferred_element_type=jnp.float32)
    content = jnp.where(is_self, self_score[:, :, None], content)
    rel_all = jnp.einsum("bhe,rhe->bhr", q_v, rel_proj, preferred_element_type=jnp.float32)
    rel_index = jnp.clip(positions[:, None] - key_steps[None, :], 0, cache_len - 1)
    rel_scores = jnp.take_along_axis(rel_all, jnp.broadcast_to(rel_index[:, None, :], rel_all.shape), axis=2)
    scores = jnp.where(is_valid, (content + rel_scores) * score_scale, -1e30)
    attn_probs = jax.nn.softmax(scores, axis=-1).astype(jnp.bfloat16)
    zero_probs = jnp.zeros_like(attn_probs)
    self_prob = jnp.sum(jnp.where(is_self, attn_probs, zero_probs), axis=-1, dtype=jnp.float32)
    cache_probs = jnp.where(is_self, zero_probs, attn_probs)
    attn_out = jnp.einsum("bhj,bhje->bhe", cache_probs, v_cache, preferred_element_type=jnp.float32)
    attn_out = attn_out + self_prob[:, :, None] * v_new.astype(jnp.float32)
    return attn_out.astype(jnp.bfloat16)


def solution(mesh):
    tok_axes = ("dp", "wg")
    in_specs = (P(tok_axes, None), P("wg"), P("wg"), P("wg", None, "tp", None), P("wg", "tp", None), P("tp", None, "wg"), P("wg", "tp"), P("tp", "wg"), P("tp", None), P("tp", None), P(None, None), P(tok_axes, "tp", None, None), P(tok_axes, "tp", None, None), P(tok_axes))
    out_specs = (P(tok_axes, None), P(tok_axes, "tp", None), P(tok_axes, "tp", None))

    def device_step(tokens, gain_attn, gain_mlp, w_qkv, w_rel, w_out, w_up, w_down, bias_u, bias_v, rel_table, k_cache, v_cache, positions):
        gain_attn_full = lax.all_gather(gain_attn, "wg", axis=0, tiled=True)
        gain_mlp_full = lax.all_gather(gain_mlp, "wg", axis=0, tiled=True)
        qkv_full = lax.all_gather(w_qkv, "wg", axis=0, tiled=True)
        rel_full = lax.all_gather(w_rel, "wg", axis=0, tiled=True)
        out_full = lax.all_gather(w_out, "wg", axis=2, tiled=True)
        up_full = lax.all_gather(w_up, "wg", axis=0, tiled=True)
        down_full = lax.all_gather(w_down, "wg", axis=1, tiled=True)
        normed = rms_norm(tokens, gain_attn_full)
        qkv_heads = jnp.einsum("td,dshe->tshe", normed, qkv_full, preferred_element_type=jnp.float32).astype(jnp.bfloat16)
        q_heads = qkv_heads[:, 0]
        k_new = qkv_heads[:, 1]
        v_new = qkv_heads[:, 2]
        rel_proj = jnp.einsum("rd,dhe->rhe", rel_table, rel_full, preferred_element_type=jnp.float32).astype(jnp.bfloat16)
        q_u = (q_heads.astype(jnp.float32) + bias_u).astype(jnp.bfloat16)
        q_v = (q_heads.astype(jnp.float32) + bias_v).astype(jnp.bfloat16)
        attn_out = cache_attention(q_u, q_v, k_new, v_new, k_cache, v_cache, positions, rel_proj)
        attn_part = jnp.einsum("the,hed->td", attn_out, out_full, preferred_element_type=jnp.float32).astype(jnp.bfloat16)
        attn_sum = lax.psum(attn_part, "tp")
        resid = tokens.astype(jnp.float32) + attn_sum.astype(jnp.float32)
        normed_mlp = rms_norm(resid, gain_mlp_full)
        hidden = jax.nn.gelu(jnp.dot(normed_mlp, up_full, preferred_element_type=jnp.float32), approximate=True).astype(jnp.bfloat16)
        mlp_part = jnp.dot(hidden, down_full, preferred_element_type=jnp.float32).astype(jnp.bfloat16)
        mlp_sum = lax.psum(mlp_part, "tp")
        layer_out = (resid + mlp_sum.astype(jnp.float32)).astype(jnp.bfloat16)
        return layer_out, k_new, v_new

    return jax.shard_map(device_step, mesh=mesh, in_specs=in_specs, out_specs=out_specs, check_vma=False)
```

profile of v0, /device:TPU:0, one launch (start us, length us, event | category | flops | bytes accessed | tf_op | source)
XLA Modules:
  0.0 692.2 jit_solution(3435802268207372699)
XLA Ops:
  7.3 2.2 copy.26
  9.5 0.7 iota_compare_fusion.1
  10.3 0.8 copy.28
  11.0 0.7 fusion.42
  11.7 0.8 copy.29
  12.6 0.9 copy.30
  13.4 0.7 shift-left_or_fusion
  14.1 1.1 copy.33
  15.3 0.4 reshape.90
  15.7 1.1 copy.31
  16.8 0.8 copy.24
  17.6 0.8 copy.25
  18.3 1.1 copy.35
  19.4 0.6 dynamic-slice
  20.7 0.3 dynamic-update-slice
  20.9 0.3 dynamic-update-slice.1
  21.2 27.6 %all-reduce.2 = (f32[2560]{0:T(1024)S(1)}, f32[2560]{0:T(1024)}) all-reduce(f32[2560]{0:T(1024)S(1)} %dynamic-update-slice, f32[2560]{0:T(1024)S(1)} %dynamic-update-slice.1), channel_id=1, replica_groups=mesh['dp'=1,'tp'=16,'wg'=8] {'wg'}, use_global_device_ids=true, to_apply=%add | all-reduce | flops 5120 | bytes 40960
  48.9 0.6 fusion.2
  49.5 14.3 %all_gather.23 = bf16[2560,2,80]{2,1,0:T(2,128)(2,1)} all-gather(bf16[320,2,80]{2,1,0:T(2,128)(2,1)S(1)} %copy.31), channel_id=1, replica_groups=mesh['dp'=1,'tp'=16,'wg'=8] {'wg'}, dimensions={0}, use_global_device_ids=true | all-gather | bytes 921600 | tf_op jit(solution)/shard_map/all_gather | solution.py:46
  63.8 14.7 %all_gather.24 = bf16[2,80,2560]{1,0,2:T(2,128)(2,1)} all-gather(bf16[2,80,320]{1,0,2:T(2,128)(2,1)S(1)} %copy.35), channel_id=1, replica_groups=mesh['dp'=1,'tp'=16,'wg'=8] {'wg'}, dimensions={2}, use_global_device_ids=true | all-gather | bytes 921600 | tf_op jit(solution)/shard_map/all_gather | solution.py:47
  78.5 8.8 %copy.27 = bf16[2560,3,2,80]{0,3,2,1:T(8,128)(2,1)} copy(bf16[2560,3,2,80]{3,2,1,0:T(2,128)(2,1)} %all-gather.4.cloned.1.call-done) | data formatting | bytes 4915200 | tf_op jit(solution)/shard_map/all_gather | solution.py:45
  87.3 3.2 fusion.6
  90.6 0.1 convert_element_type.61
  90.6 0.7 slice_bitcast_fusion
  91.4 0.1 copy-done.3
  91.5 1.8 convolution_bitcast_fusion
  93.3 313.4 %gather_fusion = f32[32768]{0:T(1024)S(1)} fusion(f32[512,2,32]{0,2,1:T(8,128)S(1)} %convolution_bitcast_fusion, s32[32768]{0:T(1024)S(1)} %reshape.90), kind=kCustom, calls=%fused_computation | custom fusion | bytes 655360 | tf_op jit(solution)/shard_map/jit(take_along_axis)/gather | solution.py:26
  406.7 0.4 reshape.93
  407.2 0.7 multiply_reduce_fusion.3
  407.9 4.1 multiply_reduce_fusion.1
  412.0 0.2 copy.48
  412.3 0.1 copy.41
  412.5 2.6 fusion.35
  415.1 0.6 convert_reduce_fusion
  415.7 0.1 copy.34
  415.8 0.2 copy.56
  416.0 3.7 multiply_reduce_fusion
  419.8 3.9 bitcast_convert_fusion
  423.8 0.7 all-gather.6.cloned.1.call-update
  424.5 0.5 all-gather.8.cloned.1.call-update
  425.1 0.3 all-reduce.8.cloned.1.call-start
  425.3 92.7 %all-reduce.6.cloned.1.call-done = bf16[512,2560]{1,0:T(8,128)(2,1)} async-done(((bf16[512,2560]{1,0:T(8,128)(2,1)}), bf16[512,2560]{1,0:T(8,128)(2,1)}) %all-reduce.6.cloned.1.call-update) | async-done | bytes 2621456 | tf_op jit(solution)/shard_map/psum | solution.py:60
  518.1 2.7 multiply_reduce_fusion.2
  520.7 26.3 %all-gather.6.cloned.1.call-done = bf16[2560,640]{1,0:T(8,128)(2,1)} async-done(((bf16[320,640]{1,0:T(8,128)(2,1)}), bf16[2560,640]{1,0:T(8,128)(2,1)}) %all-gather.6.cloned.1.call-update) | async-done | bytes 3276816 | tf_op jit(solution)/shard_map/all_gather | solution.py:48
  547.0 29.5 %all-gather.8.cloned.1.call-done = bf16[640,2560]{0,1:T(8,128)(2,1)} async-done(((bf16[640,320]{0,1:T(8,128)(2,1)}), bf16[640,2560]{0,1:T(8,128)(2,1)}) %all-gather.8.cloned.1.call-update) | async-done | bytes 3276816 | tf_op jit(solution)/shard_map/all_gather | solution.py:49
  576.6 10.9 %convolution_convert_fusion = bf16[512,2560]{1,0:T(8,128)(2,1)} fusion(bf16[640,2560]{0,1:T(8,128)(2,1)} %all-gather.8.cloned.1.call-done, bf16[2560,640]{1,0:T(8,128)(2,1)} %all-gather.6.cloned.1.call-done, bf16[512,2560]{1,0:T(8,128)(2,1)} %all-reduce.6.cloned.1.call-done, bf16[512,2560]{1,0:T(8,128)(2,1)S(1)} %copy-done.2, f32[2560]{0:T(1024)S(1)} %copy-done.15, ...), kind=kOutput, calls=%fused_computation.15 | convolution fusion | flops 3367567360 | bytes 14430208 | tf_op jit(solution)/shard_map/dot_general | solution.py:64
  587.5 93.3 %all-reduce.8.cloned.1.call-done = bf16[512,2560]{1,0:T(8,128)(2,1)} async-done(((bf16[512,2560]{1,0:T(8,128)(2,1)}), bf16[512,2560]{1,0:T(8,128)(2,1)}) %all-reduce.8.cloned.1.call-update) | async-done | bytes 2621456 | tf_op jit(solution)/shard_map/psum | solution.py:65
  680.7 5.0 add_convert_fusion
  (45 shorter events, 0.3 us)
Async XLA Ops:
  7.2 84.3 %copy-start = (bf16[32,2560]{1,0:T(8,128)(2,1)S(1)}, bf16[32,2560]{1,0:T(8,128)(2,1)}, u32[]{:S(2)}) copy-start(bf16[32,2560]{1,0:T(8,128)(2,1)} %param.24) | copy-start | bytes 491524
  7.2 12.2 %copy-start.16 = (u32[128]{0:T(128)S(1)}, u32[128]{0:T(128)}, u32[]{:S(2)}) copy-start(u32[128]{0:T(128)} %constant.71) | copy-start | bytes 1540
  7.2 13.5 %copy-start.11 = (f32[320]{0:T(512)S(1)}, f32[320]{0:T(512)}, u32[]{:S(2)}) copy-start(f32[320]{0:T(512)} %param.15) | copy-start | bytes 3844
  7.2 13.7 %copy-start.12 = (f32[320]{0:T(512)S(1)}, f32[320]{0:T(512)}, u32[]{:S(2)}) copy-start(f32[320]{0:T(512)} %param.16) | copy-start | bytes 3844
  7.2 41.7 %copy-start.1 = (bf16[512,2560]{1,0:T(8,128)(2,1)S(1)}, bf16[512,2560]{1,0:T(8,128)(2,1)}, u32[]{:S(2)}) copy-start(bf16[512,2560]{1,0:T(8,128)(2,1)} %param.14) | copy-start | bytes 7864324
  7.2 71.3 %all-gather.4.cloned.1.call-start = ((), (), s32[]{:S(2)}) async-start(), calls=%async_computation | async-start | bytes 4423680 | tf_op jit(solution)/shard_map/all_gather | solution.py:45
  9.5 508.6 %all-reduce.6.cloned.1.call-start = ((), (), s32[]{:S(2)}) async-start(), calls=%async_computation.1 | async-start | bytes 5242880 | tf_op jit(solution)/shard_map/psum | solution.py:60
  87.3 4.2 copy-start.13
  90.6 0.8 copy-start.3
  93.3 313.9 %copy-start.4 = (bf16[512,3,2,80]{0,3,2,1:T(8,128)(2,1)S(1)}, bf16[512,3,2,80]{0,3,2,1:T(8,128)(2,1)}, u32[]{:S(2)}) copy-start(bf16[512,3,2,80]{0,3,2,1:T(8,128)(2,1)} %copy-done.3) | copy-start | bytes 1474564
  93.3 313.9 %copy-start.14 = (f32[2,80]{1,0:T(2,128)S(1)}, f32[2,80]{1,0:T(2,128)}, u32[]{:S(2)}) copy-start(f32[2,80]{1,0:T(2,128)} %param.22) | copy-start | bytes 1924
  407.9 4.5 copy-start.6
  407.9 4.5 copy-start.7
  407.9 4.6 copy-start.8
  407.9 4.6 copy-start.9
  407.9 4.6 copy-start.10
  415.7 4.1 copy-start.5
  419.8 98.3 %copy-start.2 = (bf16[512,2560]{1,0:T(8,128)(2,1)S(1)}, bf16[512,2560]{1,0:T(8,128)(2,1)}, u32[]{:S(2)}) copy-start(bf16[512,2560]{1,0:T(8,128)(2,1)} %param.14) | copy-start | bytes 7864324
  423.8 152.8 %copy-start.15 = (f32[2560]{0:T(1024)S(1)}, f32[2560]{0:T(1024)}, u32[]{:S(2)}) copy-start(f32[2560]{0:T(1024)} %get-tuple-element.4) | copy-start | bytes 30724
  423.8 123.3 %all-gather.6.cloned.1.call-start = ((), (), s32[]{:S(2)}) async-start(), calls=%async_computation.2 | async-start | bytes 3686400 | tf_op jit(solution)/shard_map/all_gather | solution.py:48
  424.5 152.1 %all-gather.8.cloned.1.call-start = ((), (), s32[]{:S(2)}) async-start(), calls=%async_computation.3 | async-start | bytes 3686400 | tf_op jit(solution)/shard_map/all_gather | solution.py:49
  425.1 255.6 %all-reduce.8.cloned.1.call-start = ((), (), s32[]{:S(2)}) async-start(), calls=%async_computation.4 | async-start | bytes 5242880 | tf_op jit(solution)/shard_map/psum | solution.py:65
Sparse Core Ops, SparseCore 0:
  10.3 33.4 all-gather.3
  423.9 94.1 all-reduce.5
  519.8 27.2 all-gather.5
  548.6 27.9 all-gather.7
  587.6 93.0 all-reduce.7
where the time goes:
time: 693 us; the launch traced here: 692 us
  local copies, waits for them, and re-layouts  335 us (48%)
  waiting for transfers between devices  243 us (35%)
  blocking collectives  56.7 us (8%)
  other arithmetic  22.2 us (3%)
  matrix products  19.8 us (3%)
  between operations  14.7 us (2%)
    gather x4, local copies, waits for them, and re-layouts, cache_attention(): jnp.take_along_axis(rel_all, jnp.broadcast_to(rel_index[:, None, :], rel_...  315 us
    psum x1, waiting for transfers between devices, device_step(): mlp_sum = lax.psum(mlp_part, 'tp')  93.3 us
    psum x1, waiting for transfers between devices, device_step(): attn_sum = lax.psum(attn_part, 'tp')  92.7 us
    all_gather x1, waiting for transfers between devices, device_step(): down_full = lax.all_gather(w_down, 'wg', axis=1, tiled=True)  29.5 us
    unnamed x1, blocking collectives  27.6 us
    all_gather x1, waiting for transfers between devices, device_step(): up_full = lax.all_gather(w_up, 'wg', axis=0, tiled=True)  26.3 us
    all_gather x1, blocking collectives, device_step(): out_full = lax.all_gather(w_out, 'wg', axis=2, tiled=True)  14.7 us
    all_gather x1, blocking collectives, device_step(): rel_full = lax.all_gather(w_rel, 'wg', axis=0, tiled=True)  14.3 us
  transfers between devices with their start and end apart: 5, of which 4 were waited for; matrix products, arithmetic and copies ran while one was open for 2% of the time, Pallas kernels for 0%

commit v1 on v0

--- a/solution.py
+++ b/solution.py
@@ -23,7 +23,8 @@
     content = jnp.where(is_self, self_score[:, :, None], content)
     rel_all = jnp.einsum("bhe,rhe->bhr", q_v, rel_proj, preferred_element_type=jnp.float32)
     rel_index = jnp.clip(positions[:, None] - key_steps[None, :], 0, cache_len - 1)
-    rel_scores = jnp.take_along_axis(rel_all, jnp.broadcast_to(rel_index[:, None, :], rel_all.shape), axis=2)
+    picked = rel_index[:, :, None] == key_steps[None, None, :]
+    rel_scores = jnp.sum(jnp.where(picked[:, None], rel_all[:, :, None, :], 0.0), axis=3)
     scores = jnp.where(is_valid, (content + rel_scores) * score_scale, -1e30)
     attn_probs = jax.nn.softmax(scores, axis=-1).astype(jnp.bfloat16)
     zero_probs = jnp.zeros_like(attn_probs)
@@ -40,8 +41,8 @@
     out_specs = (P(tok_axes, None), P(tok_axes, "tp", None), P(tok_axes, "tp", None))
 
     def device_step(tokens, gain_attn, gain_mlp, w_qkv, w_rel, w_out, w_up, w_down, bias_u, bias_v, rel_table, k_cache, v_cache, positions):
-        gain_attn_full = lax.all_gather(gain_attn, "wg", axis=0, tiled=True)
-        gain_mlp_full = lax.all_gather(gain_mlp, "wg", axis=0, tiled=True)
+        gains = lax.all_gather(jnp.stack([gain_attn, gain_mlp]), "wg", axis=1, tiled=True)
+        gain_attn_full, gain_mlp_full = gains[0], gains[1]
         qkv_full = lax.all_gather(w_qkv, "wg", axis=0, tiled=True)
         rel_full = lax.all_gather(w_rel, "wg", axis=0, tiled=True)
         out_full = lax.all_gather(w_out, "wg", axis=2, tiled=True)

time: 693 us -> 358 us (0.52)
  local copies, waits for them, and re-layouts: 335 us -> 14.7 us
  blocking collectives: 56.7 us -> 45.2 us
    gather x4 -> x0, local copies, waits for them, and re-layouts: 315 us -> none  [cache_attention(): jnp.take_along_axis(rel_all, jnp.broadcast_to(rel_index[:, None, :], rel_...]
    unnamed x1 -> x0, blocking collectives: 27.6 us -> none
    all_gather x0 -> x1, blocking collectives: none -> 13.2 us  [device_step(): lax.all_gather(jnp.stack([gain_attn, gain_mlp]), 'wg', axis=1, tiled=True)]
  transfers between devices with their start and end apart: 5 -> 5, of which waited for: 4 -> 4; matrix products, arithmetic and copies ran while one was open for 2% -> 3% of each run, Pallas kernels for 0% -> 0%
where the time goes in v1:
time: 358 us
  waiting for transfers between devices  244 us (68%)
  blocking collectives  45.2 us (13%)
  other arithmetic  20.8 us (6%)
  matrix products  19.2 us (5%)
  local copies, waits for them, and re-layouts  14.7 us (4%)
  between operations  13.9 us (4%)
    psum x1, waiting for transfers between devices, device_step(): mlp_sum = lax.psum(mlp_part, 'tp')  93.3 us
    psum x1, waiting for transfers between devices, device_step(): attn_sum = lax.psum(attn_part, 'tp')  93.2 us
    all_gather x1, waiting for transfers between devices, device_step(): down_full = lax.all_gather(w_down, 'wg', axis=1, tiled=True)  29.5 us
    all_gather x1, waiting for transfers between devices, device_step(): up_full = lax.all_gather(w_up, 'wg', axis=0, tiled=True)  26.3 us
    all_gather x1, blocking collectives, device_step(): rel_full = lax.all_gather(w_rel, 'wg', axis=0, tiled=True)  17.9 us
    all_gather x1, blocking collectives, device_step(): out_full = lax.all_gather(w_out, 'wg', axis=2, tiled=True)  14.1 us
    all_gather x1, blocking collectives, device_step(): lax.all_gather(jnp.stack([gain_attn, gain_mlp]), 'wg', axis=1, tiled=True)  13.2 us
    dot_general x1, matrix products, device_step(): jnp.dot(hidden, down_full, preferred_element_type=jnp.float32)  10.8 us
  transfers between devices with their start and end apart: 5, of which 4 were waited for; matrix products, arithmetic and copies ran while one was open for 3% of the time, Pallas kernels for 0%

profile of v1, /device:TPU:0, one launch (start us, length us, event | category | flops | bytes accessed | tf_op | source)
XLA Modules:
  0.0 357.7 jit_solution(7449064366057521147)
XLA Ops:
  7.2 0.0 copy-start
  7.2 0.0 copy-start.4
  7.2 0.0 all-gather.5.cloned.1.call-start
  7.2 2.0 copy.28
  9.3 0.0 all-gather.5.cloned.1.call-update
  9.3 0.0 all-reduce.3.cloned.1.call-start
  9.4 0.7 stack.10
  10.0 0.7 stack.9
  10.7 13.2 %all-gather = f32[8,320,2]{1,2,0:T(2,128)S(1)} all-gather(f32[1,320,2]{1,2,0:T(2,128)S(1)} %maximum_bitcast_fusion), channel_id=1, replica_groups=mesh['dp'=1,'tp'=16,'wg'=8] {'wg'}, dimensions={0}, use_global_device_ids=true | all-gather | bytes 23040 | tf_op jit(solution)/shard_map/all_gather | solution.py:44
  23.9 0.1 reshape.88
  24.0 1.1 copy.30
  25.1 1.1 copy.32
  26.2 0.1 slice_reduce_fusion
  26.2 2.3 fusion.2
  28.5 0.0 copy-done.4
  28.6 1.1 iota_compare_fusion
  29.7 17.9 %all_gather.20 = bf16[2560,2,80]{2,1,0:T(2,128)(2,1)} all-gather(bf16[320,2,80]{2,1,0:T(2,128)(2,1)S(1)} %copy.30), channel_id=1, replica_groups=mesh['dp'=1,'tp'=16,'wg'=8] {'wg'}, dimensions={0}, use_global_device_ids=true | all-gather | bytes 921600 | tf_op jit(solution)/shard_map/all_gather | solution.py:47
  47.6 14.1 %all_gather.21 = bf16[2,80,2560]{1,0,2:T(2,128)(2,1)} all-gather(bf16[2,80,320]{1,0,2:T(2,128)(2,1)S(1)} %copy.32), channel_id=1, replica_groups=mesh['dp'=1,'tp'=16,'wg'=8] {'wg'}, dimensions={2}, use_global_device_ids=true | all-gather | bytes 921600 | tf_op jit(solution)/shard_map/all_gather | solution.py:48
  61.8 9.0 %copy.29 = bf16[2560,3,2,80]{0,3,2,1:T(8,128)(2,1)} copy(bf16[2560,3,2,80]{3,2,1,0:T(2,128)(2,1)} %all-gather.5.cloned.1.call-done) | data formatting | bytes 4915200 | tf_op jit(solution)/shard_map/all_gather | solution.py:46
  70.7 0.0 copy-done.1
  70.7 0.0 slice-start.1
  70.7 3.4 fusion.6
  74.1 0.1 convert_element_type.61
  74.2 0.0 copy-start.3
  74.3 0.7 multiply_reduce_fusion.3
  75.0 0.0 slice-done.1
  75.0 0.0 copy-start.6
  75.0 2.2 multiply_reduce_fusion.1
  77.2 0.0 copy-done
  77.2 2.5 convolution_bitcast_fusion
  79.7 1.8 select_reduce_fusion
  81.5 1.0 select_convert_fusion
  82.5 3.8 %multiply_reduce_fusion = f32[512,2,80]{0,2,1:T(8,128)S(1)} fusion(bf16[512,2,32,80]{0,3,2,1:T(8,128)(2,1)} %param.26, f32[512,2,32]{0,2,1:T(8,128)S(1)} %get-tuple-element.10), kind=kLoop, calls=%fused_computation.2 | loop fusion | flops 7782400 | bytes 5701632 | tf_op jit(solution)/shard_map/bhj,bhje->bhe/dot_general | solution.py:33
  86.4 2.4 bitcast_convert_fusion
  88.8 0.0 all-reduce.3.cloned.1.call-update
  88.8 0.0 all-gather.7.cloned.1.call-start
  88.9 0.7 all-gather.7.cloned.1.call-update
  89.6 0.0 all-gather.9.cloned.1.call-start
  89.6 0.5 all-gather.9.cloned.1.call-update
  90.2 0.2 all-reduce.5.cloned.1.call-start
  90.4 93.2 %all-reduce.3.cloned.1.call-done = bf16[512,2560]{1,0:T(8,128)(2,1)} async-done(((bf16[512,2560]{1,0:T(8,128)(2,1)}), bf16[512,2560]{1,0:T(8,128)(2,1)}) %all-reduce.3.cloned.1.call-update) | async-done | bytes 2621456 | tf_op jit(solution)/shard_map/psum | solution.py:61
  183.5 2.7 multiply_reduce_fusion.2
  186.2 26.3 %all-gather.7.cloned.1.call-done = bf16[2560,640]{1,0:T(8,128)(2,1)} async-done(((bf16[320,640]{1,0:T(8,128)(2,1)}), bf16[2560,640]{1,0:T(8,128)(2,1)}) %all-gather.7.cloned.1.call-update) | async-done | bytes 3276816 | tf_op jit(solution)/shard_map/all_gather | solution.py:49
  212.5 29.5 %all-gather.9.cloned.1.call-done = bf16[640,2560]{0,1:T(8,128)(2,1)} async-done(((bf16[640,320]{0,1:T(8,128)(2,1)}), bf16[640,2560]{0,1:T(8,128)(2,1)}) %all-gather.9.cloned.1.call-update) | async-done | bytes 3276816 | tf_op jit(solution)/shard_map/all_gather | solution.py:50
  242.0 10.8 %convolution_convert_fusion = bf16[512,2560]{1,0:T(8,128)(2,1)} fusion(bf16[640,2560]{0,1:T(8,128)(2,1)} %all-gather.9.cloned.1.call-done, bf16[2560,640]{1,0:T(8,128)(2,1)} %all-gather.7.cloned.1.call-done, bf16[512,2560]{1,0:T(8,128)(2,1)} %all-reduce.3.cloned.1.call-done, bf16[512,2560]{1,0:T(8,128)(2,1)S(1)} %copy-done.1, ...), kind=kOutput, calls=%fused_computation.14 | convolution fusion | flops 3367567360 | bytes 14430208 | tf_op jit(solution)/shard_map/dot_general | solution.py:65
  252.9 0.0 all-reduce.5.cloned.1.call-update
  252.9 93.3 %all-reduce.5.cloned.1.call-done = bf16[512,2560]{1,0:T(8,128)(2,1)} async-done(((bf16[512,2560]{1,0:T(8,128)(2,1)}), bf16[512,2560]{1,0:T(8,128)(2,1)}) %all-reduce.5.cloned.1.call-update) | async-done | bytes 2621456 | tf_op jit(solution)/shard_map/psum | solution.py:66
  346.2 5.0 %add_convert_fusion = bf16[512,2560]{1,0:T(8,128)(2,1)} fusion(bf16[512,2560]{1,0:T(8,128)(2,1)} %all-reduce.5.cloned.1.call-done, bf16[512,2560]{1,0:T(8,128)(2,1)} %all-reduce.3.cloned.1.call-done, bf16[512,2560]{1,0:T(8,128)(2,1)S(1)} %copy-done.1), kind=kLoop, calls=%fused_computation.11 | loop fusion | flops 7864320 | bytes 10485760 | tf_op jit(solution)/shard_map/convert_element_type | solution.py:67
  (19 shorter events, 0.1 us)
Async XLA Ops:
  7.2 70.0 %copy-start = (bf16[32,2560]{1,0:T(8,128)(2,1)S(1)}, bf16[32,2560]{1,0:T(8,128)(2,1)}, u32[]{:S(2)}) copy-start(bf16[32,2560]{1,0:T(8,128)(2,1)} %param.24) | copy-start | bytes 491524
  7.2 21.4 %copy-start.4 = (s32[512]{0:T(512)S(1)}, s32[512]{0:T(512)}, u32[]{:S(2)}) copy-start(s32[512]{0:T(512)} %param.27) | copy-start | bytes 6148
  7.2 54.6 %all-gather.5.cloned.1.call-start = ((), (), s32[]{:S(2)}) async-start(), calls=%async_computation | async-start | bytes 4423680 | tf_op jit(solution)/shard_map/all_gather | solution.py:46
  9.3 174.2 %all-reduce.3.cloned.1.call-start = ((), (), s32[]{:S(2)}) async-start(), calls=%async_computation.1 | async-start | bytes 5242880 | tf_op jit(solution)/shard_map/psum | solution.py:61
  61.8 9.0 %copy-start.1 = (bf16[512,2560]{1,0:T(8,128)(2,1)S(1)}, bf16[512,2560]{1,0:T(8,128)(2,1)}, u32[]{:S(2)}) copy-start(bf16[512,2560]{1,0:T(8,128)(2,1)} %param.14) | copy-start | bytes 7864324
  70.7 4.2 %slice-start = ((s8[5242880]{0:T(1024)(128)(4,1)}), s8[4194304]{0:T(1024)(128)(4,1)S(1)}, s32[]{:S(2)}) async-start(s8[5242880]{0:T(1024)(128)(4,1)} %bitcast.37), calls=%async_computation.5 | async-start | bytes 8388608
  70.7 3.5 copy-start.5
  70.7 4.2 %slice-start.1 = ((s8[5242880]{0:T(1024)(128)(4,1)}), s8[1048576]{0:T(1024)(128)(4,1)S(1)}, s32[]{:S(2)}) async-start(s8[5242880]{0:T(1024)(128)(4,1)} %bitcast.37), calls=%async_computation.6 | async-start | bytes 2097152
  74.2 12.1 %copy-start.3 = (bf16[512,2,80]{0,2,1:T(8,128)(2,1)}, bf16[512,2,80]{0,2,1:T(8,128)(2,1)S(1)}, u32[]{:S(2)}) copy-start(bf16[512,2,80]{0,2,1:T(8,128)(2,1)S(1)} %slice_bitcast_fusion) | copy-start | bytes 491524
  75.0 2.2 copy-start.6
  82.5 3.9 %copy-start.2 = (bf16[2,80,2560]{1,0,2:T(2,128)(2,1)S(1)}, bf16[2,80,2560]{1,0,2:T(2,128)(2,1)}, u32[]{:S(2)}) copy-start(bf16[2,80,2560]{1,0,2:T(2,128)(2,1)} %all_gather.21) | copy-start | bytes 2457604
  88.8 123.7 %all-gather.7.cloned.1.call-start = ((), (), s32[]{:S(2)}) async-start(), calls=%async_computation.2 | async-start | bytes 3686400 | tf_op jit(solution)/shard_map/all_gather | solution.py:49
  89.6 152.5 %all-gather.9.cloned.1.call-start = ((), (), s32[]{:S(2)}) async-start(), calls=%async_computation.3 | async-start | bytes 3686400 | tf_op jit(solution)/shard_map/all_gather | solution.py:50
  90.2 256.0 %all-reduce.5.cloned.1.call-start = ((), (), s32[]{:S(2)}) async-start(), calls=%async_computation.4 | async-start | bytes 5242880 | tf_op jit(solution)/shard_map/psum | solution.py:66
Sparse Core Ops, SparseCore 0:
  10.3 38.4 all-gather.4
  89.0 94.5 all-reduce.2
  185.2 27.2 all-gather.6
  214.1 27.9 all-gather.8
  253.0 93.0 all-reduce.4

commit v2 on v0

v2 whole, which is shorter than its diff:
```python
import jax
import jax.numpy as jnp
from jax import lax
from jax.experimental import pallas as pl
from jax.experimental.pallas import tpu as pltpu
from jax.sharding import PartitionSpec as P

NORM_EPS = 1e-6
BF = jnp.bfloat16
F32 = jnp.float32
MESH = pl.DeviceIdType.MESH
ANY = pl.ANY
SEQ, DM, HALF, HD, CL, FF = 512, 2560, 1280, 80, 32, 640
NT = (((1,), (1,)), ((), ()))
NN = (((1,), (0,)), ((), ()))
TN = (((0,), (0,)), ((), ()))


def mm(a, b, dims):
    return lax.dot_general(a, b, dims, preferred_element_type=F32)


def layer_kernel(x_h, pos_h, bias_h, gain_h, wq_h, wo_h, wu_h, wd_h, rt_h, k_h, v_h,
                 y_h, kn_h, vn_h,
                 x_s, pos_s, bias_s, rt_s, wg_s, wq_s, wo_s, wu_s, wd_s, k_s, v_s,
                 rs_s, acc, qt_s, qu_s, sc_s, ot_s, o_s, wof_s, kn_s, vn_s, p_s,
                 rel1, rcv1, stg1, rel2, rcv2, stg2, s2_s, h_s, g_s, u_s, hid_s,
                 lsem, gsem_s, gsem_r, rsem_s, rsem_r, asem_s, asem_r):
    tp, wg = lax.axis_index("tp"), lax.axis_index("wg")
    z, y = tp // 4, tp % 4
    x, c = wg // 2, wg % 2

    def up1(i, d):
        return lax.rem(i + d, 4)

    def dev(dz=0, dy=0, dx=0, flip=False):
        cc = 1 - c if flip else c
        return (0, up1(z, dz) * 4 + up1(y, dy), up1(x, dx) * 2 + cc)

    xp, xm, sib = dev(dx=1), dev(dx=3), dev(flip=True)
    zp, zm, yp, ym = dev(dz=1), dev(dz=3), dev(dy=1), dev(dy=3)

    sends = []

    def send(src, dst, ssem, rsem, device):
        cp = pltpu.make_async_remote_copy(src, dst, ssem, rsem, device_id=device, device_id_type=MESH)
        cp.start()
        sends.append(cp)

    def arrived(dst, ssem, rsem, device):
        pltpu.make_async_remote_copy(dst, dst, ssem, rsem, device_id=device, device_id_type=MESH).wait_recv()

    n_local = [0]

    def local(src, dst):
        cp = pltpu.make_async_copy(src, dst, lsem.at[n_local[0]])
        n_local[0] += 1
        cp.start()
        return cp

    own = 2 * x + c
    l_g = local(gain_h, wg_s.at[own])
    l_q = local(wq_h, wq_s.at[own])
    l_x = local(x_h, x_s)
    l_rt = local(rt_h, rt_s)
    l_pos = local(pos_h, pos_s)
    l_bias = local(bias_h, bias_s)
    l_wo = local(wo_h, wo_s.at[own])
    l_wu = local(wu_h, wu_s.at[own])
    l_wd = local(wd_h, wd_s.at[own])
    l_k = local(k_h, k_s)
    l_v = local(v_h, v_s)

    barrier = pltpu.get_barrier_semaphore()
    for d in (xp, xm, sib, zp, zm, yp, ym):
        pl.semaphore_signal(barrier, inc=1, device_id=d, device_id_type=MESH)
    pl.semaphore_wait(barrier, 7)

    def slot(dx, flip=False):
        return 2 * up1(x, dx) + (1 - c if flip else c)

    class Gather:
        def __init__(self, ar, buf, rows, split=True):
            self.ar, self.buf, self.rows, self.split = ar, buf, rows, split

        def ref(self, s, part):
            if part is None:
                return self.buf.at[s]
            n = self.rows // 2
            return self.buf.at[s, pl.ds(part * n, n)]

        def sems(self, k):
            return gsem_s.at[self.ar, k], gsem_r.at[self.ar, k]

        def put(self, k, s, part, device):
            r = self.ref(s, part)
            send(r, r, *self.sems(k), device)

        def got(self, k, s, part, device):
            arrived(self.ref(s, part), *self.sems(k), device)

        def start(self):
            o = slot(0)
            if self.split:
                self.put(0, o, 0, xp)
                self.put(2, o, 1, xm)
                self.put(1, o, 1, xp)
                self.put(3, o, 0, xm)
            else:
                self.put(0, o, None, xp)
                self.put(2, o, None, xm)
            self.put(6, o, None, sib)

        def forward(self):
            if self.split:
                self.got(0, slot(3), 0, xm)
                self.put(4, slot(3), 0, xp)
                self.got(2, slot(1), 1, xp)
                self.put(5, slot(1), 1, xm)
                self.got(1, slot(3), 1, xm)
                self.got(3, slot(1), 0, xp)
            else:
                self.got(0, slot(3), None, xm)
                self.put(4, slot(3), None, xp)
                self.got(2, slot(1), None, xp)
            self.put(7, slot(3), None, sib)
            self.put(8, slot(1), None, sib)

        def last(self):
            if self.split:
                self.got(4, slot(2), 0, xm)
                self.got(5, slot(2), 1, xp)
            else:
                self.got(4, slot(2), None, xm)
            self.put(9, slot(2), None, sib)

        def sibling(self, k):
            self.got(k, slot({6: 0, 7: 3, 8: 1, 9: 2}[k], True), None, sib)

    g_g = Gather(0, wg_s, 8, split=False)
    g_q = Gather(1, wq_s, 640)
    g_o = Gather(2, wo_s, 160)
    g_u = Gather(3, wu_s, 320)
    g_d = Gather(4, wd_s, 320)

    l_g.wait()
    g_g.start()
    l_q.wait()
    g_q.start()

    l_x.wait()

    def stat_rows(r, carry):
        rows = pl.ds(pl.multiple_of(r * 32, 32), 32)
        v = x_s[rows, :].astype(F32)
        ms = jnp.sum(v * v, axis=1, keepdims=True) * (1.0 / DM)
        rs_s[rows, :] = jnp.broadcast_to(lax.rsqrt(ms + NORM_EPS), (32, 128))
        return carry

    lax.fori_loop(0, 16, stat_rows, 0)
    l_rt.wait()
    acc[...] = jnp.zeros_like(acc)
    qt_s[...] = jnp.zeros_like(qt_s)
    u_s[...] = jnp.zeros_like(u_s)

    def qkv_block(dx, flip):
        s = slot(dx, flip)
        xo, co = s // 2, s % 2
        cols = pl.ds(pl.multiple_of(xo * 640 + co * 256, 128), 384)
        n_win = (x_s[:, cols].astype(F32) * rs_s[:, 0:1] * wg_s[s, 0:1, :]).astype(BF)
        acc[...] += mm(wq_s[s, 0:480, :], n_win, NT)
        qt_s[...] += mm(wq_s[s, 480:640, :], rt_s[:, cols], NT)

    qkv_block(0, False)
    g_g.forward()
    g_g.last()
    for k in (6, 7, 8, 9):
        g_g.sibling(k)
    g_q.sibling(6)
    qkv_block(0, True)
    g_q.forward()
    l_wo.wait()
    g_o.start()
    l_wu.wait()
    g_u.start()
    l_wd.wait()
    g_d.start()
    qkv_block(3, False)
    qkv_block(1, False)
    g_q.sibling(7)
    qkv_block(3, True)
    g_q.sibling(8)
    qkv_block(1, True)
    g_q.last()
    qkv_block(2, False)
    g_q.sibling(9)
    qkv_block(2, True)

    kn_s[...] = acc[160:320, :].astype(BF)
    vn_s[...] = acc[320:480, :].astype(BF)
    l_kn = local(kn_s, kn_h)
    l_vn = local(vn_s, vn_h)
    l_pos.wait()
    l_bias.wait()

    flip_rows = (lax.broadcasted_iota(jnp.int32, (CL, CL), 0) + lax.broadcasted_iota(jnp.int32, (CL, CL), 1)) % CL == 0
    flip_mat = jnp.where(flip_rows, 1.0, 0.0).astype(BF)
    rel_rev = mm(qt_s[...].astype(BF), flip_mat, NN).astype(BF)
    pos = pos_s[...]
    steps = lax.broadcasted_iota(jnp.int32, (CL, SEQ), 0)
    is_self = steps == pos
    l_k.wait()
    l_v.wait()
    g_o.forward()

    for h in range(2):
        hr = slice(h * HD, h * HD + HD)
        q = acc[hr, :].astype(BF).astype(F32)
        q_u = (q + bias_s[hr, 0:1]).astype(BF).astype(F32)
        q_v = (q + bias_s[hr, 1:2]).astype(BF)
        qu_s[...] = q_u
        rel = mm(rel_rev[hr, :], q_v, TN)
        for b in range(5):
            rel = jnp.where((pos >> b) & 1 == 1, pltpu.roll(rel, 1 << b, 0), rel)
        self_score = jnp.sum(q_u * kn_s[hr, :].astype(F32), axis=0, keepdims=True)
        for lc in range(4):
            ln = slice(lc * 128, lc * 128 + 128)
            quc = qu_s[:, ln]

            def content(g, carry, h=h, ln=ln, quc=quc):
                rows = [jnp.sum(k_s[h, g * 8 + j, :, ln].astype(F32) * quc, axis=0, keepdims=True) for j in range(8)]
                sc_s[pl.ds(pl.multiple_of(g * 8, 8), 8), ln] = jnp.concatenate(rows, axis=0)
                return carry

            lax.fori_loop(0, CL // 8, content, 0)
        scores = jnp.where(is_self, self_score, sc_s[...])
        scores = jnp.where(steps <= pos, (scores + rel) * (HD ** -0.5), -1e30)
        e = jnp.exp(scores - jnp.max(scores, axis=0, keepdims=True))
        prob = (e / jnp.sum(e, axis=0, keepdims=True)).astype(BF).astype(F32)
        self_prob = jnp.sum(jnp.where(is_self, prob, 0.0), axis=0, keepdims=True)
        sc_s[...] = jnp.where(is_self, 0.0, prob)
        for lc in range(4):
            ln = slice(lc * 128, lc * 128 + 128)

            def mix(g, o, h=h, ln=ln):
                pr = sc_s[pl.ds(pl.multiple_of(g * 8, 8), 8), ln]
                for j in range(8):
                    o = o + pr[j:j + 1, :] * v_s[h, g * 8 + j, :, ln].astype(F32)
                return o

            start = self_prob[:, ln] * vn_s[hr, ln].astype(F32)
            ot_s[hr, ln] = lax.fori_loop(0, CL // 8, mix, start)

    o_s[...] = jnp.transpose(ot_s[...]).astype(BF).reshape(4, 4, 32, 160)
    g_o.last()
    for k in (6, 7, 8, 9):
        g_o.sibling(k)
    for xo in range(4):
        even, odd = wo_s[2 * xo], wo_s[2 * xo + 1]
        base = 640 * xo
        wof_s[:, base:base + 256] = even[:, 0:256]
        wof_s[:, base + 256:base + 384] = even[:, 256:384] + odd[:, 0:128]
        wof_s[:, base + 384:base + 640] = odd[:, 128:384]

    place = ((z, y, zp, zm, yp, ym), (y, z, yp, ym, zp, zm))

    def reduce_scatter(ps, chunk, between):
        for hf in range(2):
            a, b, ap, am, _, _ = place[hf]
            ss, rr = rsem_s.at[ps, hf, 0], rsem_r.at[ps, hf, 0]
            chunk(hf, up1(a, 2))
            send(p_s.at[ps, hf, up1(a, 2), pl.ds(0, 2)], rel1.at[ps, hf, 0], ss.at[0], rr.at[0], ap)
            send(p_s.at[ps, hf, up1(a, 2), pl.ds(2, 2)], rel1.at[ps, hf, 1], ss.at[1], rr.at[1], am)
        for hf in range(2):
            a, b, ap, am, _, _ = place[hf]
            ss, rr = rsem_s.at[ps, hf, 0], rsem_r.at[ps, hf, 0]
            chunk(hf, up1(a, 1))
            send(p_s.at[ps, hf, up1(a, 1), pl.ds(2, 2)], rcv1.at[ps, hf, 0, pl.ds(2, 2)], ss.at[2], rr.at[2], ap)
            chunk(hf, up1(a, 3))
            send(p_s.at[ps, hf, up1(a, 3), pl.ds(0, 2)], rcv1.at[ps, hf, 1, pl.ds(0, 2)], ss.at[3], rr.at[3], am)
        for hf in range(2):
            chunk(hf, place[hf][0])
        for hf in range(2):
            a, b, ap, am, _, _ = place[hf]
            ss, rr = rsem_s.at[ps, hf, 0], rsem_r.at[ps, hf, 0]
            arrived(rel1.at[ps, hf, 0], ss.at[0], rr.at[0], am)
            stg1[ps, hf, 0] = (p_s[ps, hf, up1(a, 1), 0:2].astype(F32) + rel1[ps, hf, 0].astype(F32)).astype(BF)
            send(stg1.at[ps, hf, 0], rcv1.at[ps, hf, 0, pl.ds(0, 2)], ss.at[4], rr.at[4], ap)
            arrived(rel1.at[ps, hf, 1], ss.at[1], rr.at[1], ap)
            stg1[ps, hf, 1] = (p_s[ps, hf, up1(a, 3), 2:4].astype(F32) + rel1[ps, hf, 1].astype(F32)).astype(BF)
            send(stg1.at[ps, hf, 1], rcv1.at[ps, hf, 1, pl.ds(2, 2)], ss.at[5], rr.at[5], am)
        between(0)
        for hf in range(2):
            a, b, ap, am, bp, bm = place[hf]
            ss, rr = rsem_s.at[ps, hf, 0], rsem_r.at[ps, hf, 0]
            arrived(rcv1.at[ps, hf, 0, pl.ds(2, 2)], ss.at[2], rr.at[2], am)
            arrived(rcv1.at[ps, hf, 1, pl.ds(0, 2)], ss.at[3], rr.at[3], ap)
            arrived(rcv1.at[ps, hf, 0, pl.ds(0, 2)], ss.at[4], rr.at[4], am)
            arrived(rcv1.at[ps, hf, 1, pl.ds(2, 2)], ss.at[5], rr.at[5], ap)
            for j in (2, 1, 3, 0):
                bj = up1(b, j)
                s2_s[ps, hf, bj] = (p_s[ps, hf, a, bj].astype(F32) + rcv1[ps, hf, 0, bj].astype(F32)
                                    + rcv1[ps, hf, 1, bj].astype(F32)).astype(BF)
                ss, rr = rsem_s.at[ps, hf, 1], rsem_r.at[ps, hf, 1]
                if j == 2:
                    send(s2_s.at[ps, hf, bj, pl.ds(0, 16)], rel2.at[ps, hf, 0], ss.at[0], rr.at[0], bp)
                    send(s2_s.at[ps, hf, bj, pl.ds(16, 16)], rel2.at[ps, hf, 1], ss.at[1], rr.at[1], bm)
                elif j == 1:
                    send(s2_s.at[ps, hf, bj, pl.ds(16, 16)], rcv2.at[ps, hf, 0, pl.ds(16, 16)], ss.at[2], rr.at[2], bp)
                elif j == 3:
                    send(s2_s.at[ps, hf, bj, pl.ds(0, 16)], rcv2.at[ps, hf, 1, pl.ds(0, 16)], ss.at[3], rr.at[3], bm)
        for hf in range(2):
            a, b, ap, am, bp, bm = place[hf]
            ss, rr = rsem_s.at[ps, hf, 1], rsem_r.at[ps, hf, 1]
            arrived(rel2.at[ps, hf, 0], ss.at[0], rr.at[0], bm)
            stg2[ps, hf, 0] = (s2_s[ps, hf, up1(b, 1), 0:16].astype(F32) + rel2[ps, hf, 0].astype(F32)).astype(BF)
            send(stg2.at[ps, hf, 0], rcv2.at[ps, hf, 0, pl.ds(0, 16)], ss.at[4], rr.at[4], bp)
            arrived(rel2.at[ps, hf, 1], ss.at[1], rr.at[1], bp)
            stg2[ps, hf, 1] = (s2_s[ps, hf, up1(b, 3), 16:32].astype(F32) + rel2[ps, hf, 1].astype(F32)).astype(BF)
            send(stg2.at[ps, hf, 1], rcv2.at[ps, hf, 1, pl.ds(16, 16)], ss.at[5], rr.at[5], bm)
        between(1)
        out = []
        for hf in range(2):
            a, b, ap, am, bp, bm = place[hf]
            ss, rr = rsem_s.at[ps, hf, 1], rsem_r.at[ps, hf, 1]
            arrived(rcv2.at[ps, hf, 0, pl.ds(16, 16)], ss.at[2], rr.at[2], bm)
            arrived(rcv2.at[ps, hf, 1, pl.ds(0, 16)], ss.at[3], rr.at[3], bp)
            arrived(rcv2.at[ps, hf, 0, pl.ds(0, 16)], ss.at[4], rr.at[4], bm)
            arrived(rcv2.at[ps, hf, 1, pl.ds(16, 16)], ss.at[5], rr.at[5], bp)
            out.append(s2_s[ps, hf, b].astype(F32) + rcv2[ps, hf, 0].astype(F32) + rcv2[ps, hf, 1].astype(F32))
        return out

    class Ring:
        def __init__(self, ps, ph, hf):
            a, b, ap, am, bp, bm = place[hf]
            self.ps, self.ph, self.hf, self.a = ps, ph, hf, a
            self.i, self.fwd, self.bwd = (b, bp, bm) if ph == 0 else (a, ap, am)

        def ref(self, d, part):
            i = up1(self.i, d)
            if self.ph == 0:
                return g_s.at[self.ps, self.hf, self.a, i, pl.ds(part * 16, 16)]
            return g_s.at[self.ps, self.hf, i, pl.ds(part * 2, 2)]

        def sems(self, k):
            return asem_s.at[self.ps, self.hf, self.ph, k], asem_r.at[self.ps, self.hf, self.ph, k]

        def put(self, k, d, part, device):
            r = self.ref(d, part)
            send(r, r, *self.sems(k), device)

        def got(self, k):
            d, part, device = {0: (3, 0, self.bwd), 1: (1, 1, self.fwd), 2: (3, 1, self.bwd),
                               3: (1, 0, self.fwd), 4: (2, 0, self.bwd), 5: (2, 1, self.fwd)}[k]
            arrived(self.ref(d, part), *self.sems(k), device)

        def start(self):
            self.put(0, 0, 0, self.fwd)
            self.put(1, 0, 1, self.bwd)
            self.put(2, 0, 1, self.fwd)
            self.put(3, 0, 0, self.bwd)

        def forward(self):
            self.got(0)
            self.put(4, 3, 0, self.fwd)
            self.got(1)
            self.put(5, 1, 1, self.bwd)

    def all_gather(ps, consume):
        inner = [Ring(ps, 0, hf) for hf in range(2)]
        outer = [Ring(ps, 1, hf) for hf in range(2)]
        for r in inner:
            r.start()
        for r in inner:
            r.forward()
        for hf in range(2):
            for k in (2, 3, 4, 5):
                inner[hf].got(k)
            outer[hf].start()
        for hf in range(2):
            consume(hf, outer[hf].i)
        for r in outer:
            r.forward()
        for k, d in ((2, 3), (3, 1)):
            for hf in range(2):
                outer[hf].got(k)
                consume(hf, up1(outer[hf].i, d))
        for hf in range(2):
            outer[hf].got(4)
            outer[hf].got(5)
            consume(hf, up1(outer[hf].i, 2))

    def out_chunk(hf, i):
        rows = (o_s[i] if hf == 0 else o_s[:, i]).reshape(128, 160)
        part = mm(rows, wof_s[:, hf * HALF:hf * HALF + HALF], NN)
        p_s[0, hf, i] = part.astype(BF).reshape(4, 32, HALF)

    def attn_between(step):
        if step == 0:
            g_u.forward()
        else:
            g_u.last()

    part = reduce_scatter(0, out_chunk, attn_between)
    mine = pl.ds(pl.multiple_of(tp * 32, 32), 32)
    for hf in range(2):
        cols = slice(hf * HALF, hf * HALF + HALF)
        h_s[:, cols] = x_s[mine, cols].astype(F32) + part[hf]
    resid = h_s[...]
    inv = lax.rsqrt(jnp.sum(resid * resid, axis=1, keepdims=True) * (1.0 / DM) + NORM_EPS)
    gains = []
    for xo in range(4):
        even, odd = wg_s[2 * xo, 1:2, :], wg_s[2 * xo + 1, 1:2, :]
        gains += [even[:, 0:256], even[:, 256:384] + odd[:, 0:128], odd[:, 128:384]]
    normed = (resid * inv * jnp.concatenate(gains, axis=1)).astype(BF)
    g_s[0, 0, z, y] = normed[:, 0:HALF]
    g_s[0, 1, y, z] = normed[:, HALF:DM]

    first = [True]

    def up_part(hf, i):
        if first[0]:
            first[0] = False
            for k in (6, 7, 8, 9):
                g_u.sibling(k)
        w = wu_s[4 * hf:4 * hf + 4].reshape(HALF, FF)
        prod = mm(g_s[0, hf, i].reshape(128, HALF), w, NN).reshape(4, 32, FF)
        if hf == 0:
            u_s[i] += prod
        else:
            u_s[:, i] += prod

    all_gather(0, up_part)
    g_d.forward()
    g_d.last()
    for k in (6, 7, 8, 9):
        g_d.sibling(k)
    for i in range(4):
        hid_s[i] = jax.nn.gelu(u_s[i], approximate=True).astype(BF)

    def down_chunk(hf, i):
        rows = (hid_s[i] if hf == 0 else hid_s[:, i]).reshape(128, FF)
        w = wd_s[4 * hf:4 * hf + 4].reshape(HALF, FF)
        p_s[1, hf, i] = mm(rows, w, NT).astype(BF).reshape(4, 32, HALF)

    part = reduce_scatter(1, down_chunk, lambda step: None)
    g_s[1, 0, z, y] = (h_s[:, 0:HALF] + part[0]).astype(BF)
    g_s[1, 1, y, z] = (h_s[:, HALF:DM] + part[1]).astype(BF)
    outs = [l_kn, l_vn]

    def write_out(hf, i):
        if hf == 0:
            outs.append(local(g_s.at[1, 0, i], y_h.at[i, :, :, pl.ds(0, HALF)]))
        else:
            outs.append(local(g_s.at[1, 1, i], y_h.at[:, i, :, pl.ds(HALF, HALF)]))

    all_gather(1, write_out)
    for cp in outs:
        cp.wait()
    for cp in sends:
        cp.wait_send()


def solution(mesh):
    tok_axes = ("dp", "wg")
    in_specs = (P(tok_axes, None), P("wg"), P("wg"), P("wg", None, "tp", None), P("wg", "tp", None), P("tp", None, "wg"), P("wg", "tp"), P("tp", "wg"), P("tp", None), P("tp", None), P(None, None), P(tok_axes, "tp", None, None), P(tok_axes, "tp", None, None), P(tok_axes))
    out_specs = (P(tok_axes, None), P(tok_axes, "tp", None), P(tok_axes, "tp", None))

    def vm(shape, dtype=BF):
        return pltpu.VMEM(shape, dtype)

    scratch = [
        vm((SEQ, DM)), vm((1, SEQ), jnp.int32), vm((160, 128), F32), vm((CL, DM)),
        vm((8, 8, 384), F32), vm((8, 640, 384)), vm((8, 160, 384)), vm((8, 320, FF)), vm((8, 320, FF)),
        vm((2, CL, HD, SEQ)), vm((2, CL, HD, SEQ)),
        vm((SEQ, 128), F32), vm((480, SEQ), F32), vm((160, CL), F32), vm((HD, SEQ), F32), vm((CL, SEQ), F32),
        vm((160, SEQ), F32), vm((4, 4, 32, 160)), vm((160, DM)), vm((160, SEQ)), vm((160, SEQ)),
        vm((2, 2, 4, 4, 32, HALF)),
        vm((2, 2, 2, 2, 32, HALF)), vm((2, 2, 2, 4, 32, HALF)), vm((2, 2, 2, 2, 32, HALF)),
        vm((2, 2, 2, 16, HALF)), vm((2, 2, 2, 32, HALF)), vm((2, 2, 2, 16, HALF)),
        vm((2, 2, 4, 32, HALF)), vm((32, DM), F32), vm((2, 2, 4, 4, 32, HALF)),
        vm((4, 4, 32, FF), F32), vm((4, 4, 32, FF)),
        pltpu.SemaphoreType.DMA((24,)),
        pltpu.SemaphoreType.DMA((5, 10)), pltpu.SemaphoreType.DMA((5, 10)),
        pltpu.SemaphoreType.DMA((2, 2, 2, 6)), pltpu.SemaphoreType.DMA((2, 2, 2, 6)),
        pltpu.SemaphoreType.DMA((2, 2, 2, 6)), pltpu.SemaphoreType.DMA((2, 2, 2, 6)),
    ]
    call = pl.pallas_call(
        layer_kernel,
        out_shape=(jax.ShapeDtypeStruct((4, 4, 32, DM), BF), jax.ShapeDtypeStruct((160, SEQ), BF), jax.ShapeDtypeStruct((160, SEQ), BF)),
        in_specs=[pl.BlockSpec(memory_space=ANY)] * 11,
        out_specs=[pl.BlockSpec(memory_space=ANY)] * 3,
        scratch_shapes=scratch,
        compiler_params=pltpu.CompilerParams(collective_id=0, has_side_effects=True, vmem_limit_bytes=62 * 1024 * 1024),
        name="layer",
    )

    def device_step(tokens, gain_attn, gain_mlp, w_qkv, w_rel, w_out, w_up, w_down, bias_u, bias_v, rel_table, k_cache, v_cache, positions):
        odd = lax.axis_index("wg") % 2 == 1

        def window(w):
            return jnp.where(odd, jnp.pad(w, ((0, 0), (64, 0))), jnp.pad(w, ((0, 0), (0, 64))))

        wq = window(jnp.concatenate([w_qkv.transpose(1, 2, 3, 0).reshape(480, 320), w_rel.transpose(1, 2, 0).reshape(160, 320)]))
        wo = window(w_out.reshape(160, 320))
        gains = window(jnp.pad(jnp.stack([gain_attn, gain_mlp]), ((0, 6), (0, 0))))
        bias = jnp.pad(jnp.stack([bias_u.reshape(160), bias_v.reshape(160)], axis=1), ((0, 0), (0, 126)))
        out, k_new, v_new = call(
            tokens, positions.reshape(1, SEQ), bias, gains, wq, wo, w_up, w_down.T, rel_table,
            k_cache.transpose(1, 2, 3, 0), v_cache.transpose(1, 2, 3, 0))
        return (out.reshape(SEQ, DM), k_new.reshape(2, HD, SEQ).transpose(2, 0, 1), v_new.reshape(2, HD, SEQ).transpose(2, 0, 1))

    return jax.shard_map(device_step, mesh=mesh, in_specs=in_specs, out_specs=out_specs, check_vma=False)
```

time: 693 us -> 156 us (0.23)
  local copies, waits for them, and re-layouts: 335 us -> 8.43 us
  waiting for transfers between devices: 243 us -> 0 us
  Pallas kernels: 0 us -> 142 us
  blocking collectives: 56.7 us -> 0 us
  matrix products: 19.8 us -> 0 us
  other arithmetic: 22.2 us -> 4.6 us
  between operations: 14.7 us -> 0.69 us
    gather x4 -> x0, local copies, waits for them, and re-layouts: 315 us -> none  [cache_attention(): jnp.take_along_axis(rel_all, jnp.broadcast_to(rel_index[:, None, :], rel_...]
    psum x2 -> x0, waiting for transfers between devices: 186 us -> none  [the longest x1 93.3 us: device_step(): mlp_sum = lax.psum(mlp_part, 'tp')]
    pallas_call x0 -> x1, Pallas kernels: none -> 142 us  [device_step(): call(tokens, positions.reshape(1, SEQ), bias, gains, wq, wo, w_up, w_down...]
    all_gather x3 -> x0, waiting for transfers between devices: 55.8 us -> none  [the longest x1 29.5 us: device_step(): down_full = lax.all_gather(w_down, 'wg', axis=1, tiled=True)]
    all_gather x2 -> x0, blocking collectives: 29 us -> none  [the longest x1 14.7 us: device_step(): out_full = lax.all_gather(w_out, 'wg', axis=2, tiled=True)]
    unnamed x1 -> x0, blocking collectives: 27.6 us -> none
    dot_general x3 -> x0, matrix products: 16.6 us -> none  [the longest x1 10.9 us: device_step(): jnp.dot(hidden, down_full, preferred_element_type=jnp.float32)]
    all_gather x1 -> x0, local copies, waits for them, and re-layouts: 8.8 us -> none  [device_step(): qkv_full = lax.all_gather(w_qkv, 'wg', axis=0, tiled=True)]
  transfers between devices with their start and end apart: 5 -> 0, of which waited for: 4 -> 0; matrix products, arithmetic and copies ran while one was open for 2% -> 0% of each run, Pallas kernels for 0% -> 0%
where the time goes in v2:
time: 156 us; the launch traced here: 155 us
  Pallas kernels  142 us (91%)
  local copies, waits for them, and re-layouts  8.43 us (5%)
  other arithmetic  4.6 us (3%)
    pallas_call x1, Pallas kernels, device_step(): call(tokens, positions.reshape(1, SEQ), bias, gains, wq, wo, w_up, w_down...  142 us
    unnamed x7, local copies, waits for them, and re-layouts  4.79 us
    select_n x3, other arithmetic, window(): jnp.where(odd, jnp.pad(w, ((0, 0), (64, 0))), jnp.pad(w, ((0, 0), (0, 64))))  3.46 us

profile of v2, /device:TPU:0, one launch (start us, length us, event | category | flops | bytes accessed | tf_op | source)
XLA Modules:
  0.0 155.3 jit_solution(14997774174446437757)
XLA Ops:
  0.6 0.8 stack_reshape.6
  1.4 0.8 stack_reshape.7
  2.2 0.7 stack.13
  2.9 0.7 stack.14
  3.6 0.7 pad_select_fusion.2.gain_h
  4.2 0.1 copy.19
  4.3 0.7 pad.32.bias_h
  5.0 1.7 %pad_select_fusion.1.wo_h = bf16[160,384]{1,0:T(8,128)(2,1)} fusion(bf16[160,320]{1,0:T(8,128)(2,1)} %bitcast.25, pred[]{:T(512)S(6)} %eq.5), kind=kLoop, calls=%fused_computation.2 | loop fusion | flops 61440 | bytes 225281 | tf_op jit(solution)/shard_map/jit(_where)/select_n | solution.py:502
  6.7 1.1 pad_maximum_fusion
  7.8 1.1 pad_select_fusion.wq_h
  8.9 141.6 %layer.1 = (bf16[4,4,32,2560]{3,2,1,0:T(8,128)(2,1)}, bf16[160,512]{1,0:T(8,128)(2,1)}, bf16[160,512]{1,0:T(8,128)(2,1)}) custom-call(bf16[512,2560]{1,0:T(8,128)(2,1)} %x_h.1, s32[1,512]{1,0:T(1,128)} %bitcast.27, f32[160,128]{1,0:T(8,128)} %pad.32.bias_h, f32[8,384]{1,0:T(8,128)} %pad_select_fusion.2.gain_h, bf16[640,384]{1,0:T(8,128)(2,1)} %pad_select_fusion.wq_h, ...), custom_call_target="tpu_custom_call" | custom-call | tf_op jit(solution)/shard_map/layer/pallas_call | solution.py:508
  150.5 0.0 copy-start.1
  150.5 0.0 copy-start
  150.5 3.4 %copy.23 = bf16[512,2560]{1,0:T(8,128)(2,1)} copy(bf16[512,2560]{1,0:T(8,128)(2,1)} %bitcast.20) | data formatting | bytes 5242880
  154.0 0.0 copy-done.1
  154.0 0.7 copy.24
  154.6 0.0 copy-done
  154.6 0.7 copy.25
  (2 shorter events, 0.0 us)
Async XLA Ops:
  150.5 3.5 %copy-start.1 = (bf16[160,512]{1,0:T(8,128)(2,1)S(1)}, bf16[160,512]{1,0:T(8,128)(2,1)}, u32[]{:S(2)}) copy-start(bf16[160,512]{1,0:T(8,128)(2,1)} %get-tuple-element.7) | copy-start | bytes 491524
  150.5 4.1 %copy-start = (bf16[160,512]{1,0:T(8,128)(2,1)S(1)}, bf16[160,512]{1,0:T(8,128)(2,1)}, u32[]{:S(2)}) copy-start(bf16[160,512]{1,0:T(8,128)(2,1)} %get-tuple-element.8) | copy-start | bytes 491524

commit v3 on v2

--- a/solution.py
+++ b/solution.py
@@ -20,10 +20,10 @@
     return lax.dot_general(a, b, dims, preferred_element_type=F32)
 
 
-def layer_kernel(x_h, pos_h, bias_h, gain_h, wq_h, wo_h, wu_h, wd_h, rt_h, k_h, v_h,
-                 y_h, kn_h, vn_h,
-                 x_s, pos_s, bias_s, rt_s, wg_s, wq_s, wo_s, wu_s, wd_s, k_s, v_s,
-                 rs_s, acc, qt_s, qu_s, sc_s, ot_s, o_s, wof_s, kn_s, vn_s, p_s,
+def layer_kernel(x_h, pos_h, bu_h, bv_h, gain_h, wq_h, wr_h, wo_h, wu_h, wd_h, rt_h, k_h, v_h,
+                 y_v, kn_s, vn_s,
+                 x_s, pos_s, bu_s, bv_s, rt_s, wr_s, wg_s, wq_s, qp_s, wo_s, wu_s, wd_s, k_s, v_s,
+                 rs_s, acc, qu_s, sc_s, ot_s, o_s, wof_s, p_s,
                  rel1, rcv1, stg1, rel2, rcv2, stg2, s2_s, h_s, g_s, u_s, hid_s,
                  lsem, gsem_s, gsem_r, rsem_s, rsem_r, asem_s, asem_r):
     tp, wg = lax.axis_index("tp"), lax.axis_index("wg")
@@ -64,7 +64,9 @@
     l_x = local(x_h, x_s)
     l_rt = local(rt_h, rt_s)
     l_pos = local(pos_h, pos_s)
-    l_bias = local(bias_h, bias_s)
+    l_bu = local(bu_h, bu_s)
+    l_bv = local(bv_h, bv_s)
+    l_wr = local(wr_h, wr_s)
     l_wo = local(wo_h, wo_s.at[own])
     l_wu = local(wu_h, wu_s.at[own])
     l_wd = local(wd_h, wd_s.at[own])
@@ -138,10 +140,11 @@
             self.got(k, slot({6: 0, 7: 3, 8: 1, 9: 2}[k], True), None, sib)
 
     g_g = Gather(0, wg_s, 8, split=False)
-    g_q = Gather(1, wq_s, 640)
+    g_q = Gather(1, wq_s, 480)
     g_o = Gather(2, wo_s, 160)
     g_u = Gather(3, wu_s, 320)
     g_d = Gather(4, wd_s, 320)
+    g_r = Gather(5, qp_s, 32)
 
     l_g.wait()
     g_g.start()
@@ -159,67 +162,74 @@
 
     lax.fori_loop(0, 16, stat_rows, 0)
     l_rt.wait()
+    l_wr.wait()
+    base = pl.multiple_of(640 * x, 128)
+    q_even = mm(rt_s[:, pl.ds(base, 384)][:, 0:320], wr_s[...], NT)
+    q_odd = mm(rt_s[:, pl.ds(pl.multiple_of(base + 256, 128), 384)][:, 64:384], wr_s[...], NT)
+    qp_s[own] = jnp.where(c == 1, q_odd, q_even)
+    g_r.start()
     acc[...] = jnp.zeros_like(acc)
-    qt_s[...] = jnp.zeros_like(qt_s)
     u_s[...] = jnp.zeros_like(u_s)
 
-    def qkv_block(dx, flip):
-        s = slot(dx, flip)
-        xo, co = s // 2, s % 2
-        cols = pl.ds(pl.multiple_of(xo * 640 + co * 256, 128), 384)
-        n_win = (x_s[:, cols].astype(F32) * rs_s[:, 0:1] * wg_s[s, 0:1, :]).astype(BF)
-        acc[...] += mm(wq_s[s, 0:480, :], n_win, NT)
-        qt_s[...] += mm(wq_s[s, 480:640, :], rt_s[:, cols], NT)
-
-    qkv_block(0, False)
+    def qkv_pair(dx):
+        xo = up1(x, dx)
+        cols = pl.ds(pl.multiple_of(xo * 640, 128), 640)
+        gain = jnp.concatenate([wg_s[2 * xo, 0:1, :], wg_s[2 * xo + 1, 0:1, :]], axis=1)
+        n_win = (x_s[:, cols].astype(F32) * rs_s[:, 0:1] * gain).astype(BF)
+        w = jnp.concatenate([wq_s[2 * xo], wq_s[2 * xo + 1]], axis=1)
+        acc[...] += mm(w, n_win, NT)
+
     g_g.forward()
     g_g.last()
     for k in (6, 7, 8, 9):
         g_g.sibling(k)
     g_q.sibling(6)
-    qkv_block(0, True)
+    qkv_pair(0)
     g_q.forward()
+    g_r.forward()
     l_wo.wait()
     g_o.start()
-    l_wu.wait()
-    g_u.start()
-    l_wd.wait()
-    g_d.start()
-    qkv_block(3, False)
-    qkv_block(1, False)
     g_q.sibling(7)
-    qkv_block(3, True)
+    qkv_pair(3)
     g_q.sibling(8)
-    qkv_block(1, True)
+    qkv_pair(1)
     g_q.last()
-    qkv_block(2, False)
+    g_r.last()
     g_q.sibling(9)
-    qkv_block(2, True)
+    qkv_pair(2)
 
     kn_s[...] = acc[160:320, :].astype(BF)
     vn_s[...] = acc[320:480, :].astype(BF)
-    l_kn = local(kn_s, kn_h)
-    l_vn = local(vn_s, vn_h)
     l_pos.wait()
-    l_bias.wait()
+    l_bu.wait()
+    l_bv.wait()
+    for k in (6, 7, 8, 9):
+        g_r.sibling(k)
 
     flip_rows = (lax.broadcasted_iota(jnp.int32, (CL, CL), 0) + lax.broadcasted_iota(jnp.int32, (CL, CL), 1)) % CL == 0
     flip_mat = jnp.where(flip_rows, 1.0, 0.0).astype(BF)
-    rel_rev = mm(qt_s[...].astype(BF), flip_mat, NN).astype(BF)
+    q_rel = qp_s[0]
+    for i in range(1, 8):
+        q_rel = q_rel + qp_s[i]
+    rel_rev = mm(flip_mat, q_rel.astype(BF), NN).astype(BF)
+    diag = lax.broadcasted_iota(jnp.int32, (HD, HD), 0) == lax.broadcasted_iota(jnp.int32, (HD, HD), 1)
+
+    def column(row):
+        return jnp.sum(jnp.where(diag, row, 0.0), axis=1, keepdims=True)
+
     pos = pos_s[...]
     steps = lax.broadcasted_iota(jnp.int32, (CL, SEQ), 0)
     is_self = steps == pos
     l_k.wait()
     l_v.wait()
-    g_o.forward()
 
     for h in range(2):
         hr = slice(h * HD, h * HD + HD)
         q = acc[hr, :].astype(BF).astype(F32)
-        q_u = (q + bias_s[hr, 0:1]).astype(BF).astype(F32)
-        q_v = (q + bias_s[hr, 1:2]).astype(BF)
+        q_u = (q + column(bu_s[h:h + 1, :])).astype(BF).astype(F32)
+        q_v = (q + column(bv_s[h:h + 1, :])).astype(BF)
         qu_s[...] = q_u
-        rel = mm(rel_rev[hr, :], q_v, TN)
+        rel = mm(rel_rev[:, hr], q_v, NN)
         for b in range(5):
             rel = jnp.where((pos >> b) & 1 == 1, pltpu.roll(rel, 1 << b, 0), rel)
         self_score = jnp.sum(q_u * kn_s[hr, :].astype(F32), axis=0, keepdims=True)
@@ -250,17 +260,19 @@
 
             start = self_prob[:, ln] * vn_s[hr, ln].astype(F32)
             ot_s[hr, ln] = lax.fori_loop(0, CL // 8, mix, start)
+        if h == 0:
+            g_o.forward()
+            l_wu.wait()
+            g_u.start()
+            l_wd.wait()
+            g_d.start()
 
     o_s[...] = jnp.transpose(ot_s[...]).astype(BF).reshape(4, 4, 32, 160)
     g_o.last()
     for k in (6, 7, 8, 9):
         g_o.sibling(k)
     for xo in range(4):
-        even, odd = wo_s[2 * xo], wo_s[2 * xo + 1]
-        base = 640 * xo
-        wof_s[:, base:base + 256] = even[:, 0:256]
-        wof_s[:, base + 256:base + 384] = even[:, 256:384] + odd[:, 0:128]
-        wof_s[:, base + 384:base + 640] = odd[:, 128:384]
+        wof_s[:, 640 * xo:640 * xo + 640] = jnp.concatenate([wo_s[2 * xo], wo_s[2 * xo + 1]], axis=1)
 
     place = ((z, y, zp, zm, yp, ym), (y, z, yp, ym, zp, zm))
 
@@ -338,9 +350,11 @@
 
         def ref(self, d, part):
             i = up1(self.i, d)
+            buf, cols = (g_s, y_v)[self.ps], pl.ds(self.hf * HALF, HALF)
+            rows = pl.ds(part * 16, 16) if self.ph == 0 else pl.ds(part * 2, 2)
             if self.ph == 0:
-                return g_s.at[self.ps, self.hf, self.a, i, pl.ds(part * 16, 16)]
-            return g_s.at[self.ps, self.hf, i, pl.ds(part * 2, 2)]
+                return buf.at[z, i, rows, cols] if self.hf == 0 else buf.at[i, y, rows, cols]
+            return buf.at[i, rows, :, cols] if self.hf == 0 else buf.at[rows, i, :, cols]
 
         def sems(self, k):
             return asem_s.at[self.ps, self.hf, self.ph, k], asem_r.at[self.ps, self.hf, self.ph, k]
@@ -396,10 +410,8 @@
         p_s[0, hf, i] = part.astype(BF).reshape(4, 32, HALF)
 
     def attn_between(step):
-        if step == 0:
+        if step == 1:
             g_u.forward()
-        else:
-            g_u.last()
 
     part = reduce_scatter(0, out_chunk, attn_between)
     mine = pl.ds(pl.multiple_of(tp * 32, 32), 32)
@@ -408,30 +420,28 @@
         h_s[:, cols] = x_s[mine, cols].astype(F32) + part[hf]
     resid = h_s[...]
     inv = lax.rsqrt(jnp.sum(resid * resid, axis=1, keepdims=True) * (1.0 / DM) + NORM_EPS)
-    gains = []
-    for xo in range(4):
-        even, odd = wg_s[2 * xo, 1:2, :], wg_s[2 * xo + 1, 1:2, :]
-        gains += [even[:, 0:256], even[:, 256:384] + odd[:, 0:128], odd[:, 128:384]]
-    normed = (resid * inv * jnp.concatenate(gains, axis=1)).astype(BF)
-    g_s[0, 0, z, y] = normed[:, 0:HALF]
-    g_s[0, 1, y, z] = normed[:, HALF:DM]
+    gain = jnp.concatenate([wg_s[i, 1:2, :] for i in range(8)], axis=1)
+    g_s[z, y] = (resid * inv * gain).astype(BF)
 
     first = [True]
 
     def up_part(hf, i):
         if first[0]:
             first[0] = False
+            g_u.last()
+            g_d.forward()
             for k in (6, 7, 8, 9):
                 g_u.sibling(k)
         w = wu_s[4 * hf:4 * hf + 4].reshape(HALF, FF)
-        prod = mm(g_s[0, hf, i].reshape(128, HALF), w, NN).reshape(4, 32, FF)
+        cols = slice(hf * HALF, hf * HALF + HALF)
+        rows = (g_s[i, :, :, cols] if hf == 0 else g_s[:, i, :, cols]).reshape(128, HALF)
+        prod = mm(rows, w, NN).reshape(4, 32, FF)
         if hf == 0:
             u_s[i] += prod
         else:
             u_s[:, i] += prod
 
     all_gather(0, up_part)
-    g_d.forward()
     g_d.last()
     for k in (6, 7, 8, 9):
         g_d.sibling(k)
@@ -444,19 +454,8 @@
         p_s[1, hf, i] = mm(rows, w, NT).astype(BF).reshape(4, 32, HALF)
 
     part = reduce_scatter(1, down_chunk, lambda step: None)
-    g_s[1, 0, z, y] = (h_s[:, 0:HALF] + part[0]).astype(BF)
-    g_s[1, 1, y, z] = (h_s[:, HALF:DM] + part[1]).astype(BF)
-    outs = [l_kn, l_vn]
-
-    def write_out(hf, i):
-        if hf == 0:
-            outs.append(local(g_s.at[1, 0, i], y_h.at[i, :, :, pl.ds(0, HALF)]))
-        else:
-            outs.append(local(g_s.at[1, 1, i], y_h.at[:, i, :, pl.ds(HALF, HALF)]))
-
-    all_gather(1, write_out)
-    for cp in outs:
-        cp.wait()
+    y_v[z, y] = jnp.concatenate([h_s[:, 0:HALF] + part[0], h_s[:, HALF:DM] + part[1]], axis=1).astype(BF)
+    all_gather(1, lambda hf, i: None)
     for cp in sends:
         cp.wait_send()
 
@@ -470,43 +469,36 @@
         return pltpu.VMEM(shape, dtype)
 
     scratch = [
-        vm((SEQ, DM)), vm((1, SEQ), jnp.int32), vm((160, 128), F32), vm((CL, DM)),
-        vm((8, 8, 384), F32), vm((8, 640, 384)), vm((8, 160, 384)), vm((8, 320, FF)), vm((8, 320, FF)),
+        vm((SEQ, DM)), vm((1, SEQ), jnp.int32), vm((2, HD), F32), vm((2, HD), F32), vm((CL, DM)), vm((160, 320)),
+        vm((8, 2, 320), F32), vm((8, 480, 320)), vm((8, CL, 160), F32), vm((8, 160, 320)), vm((8, 320, FF)), vm((8, 320, FF)),
         vm((2, CL, HD, SEQ)), vm((2, CL, HD, SEQ)),
-        vm((SEQ, 128), F32), vm((480, SEQ), F32), vm((160, CL), F32), vm((HD, SEQ), F32), vm((CL, SEQ), F32),
-        vm((160, SEQ), F32), vm((4, 4, 32, 160)), vm((160, DM)), vm((160, SEQ)), vm((160, SEQ)),
+        vm((SEQ, 128), F32), vm((480, SEQ), F32), vm((HD, SEQ), F32), vm((CL, SEQ), F32),
+        vm((160, SEQ), F32), vm((4, 4, 32, 160)), vm((160, DM)),
         vm((2, 2, 4, 4, 32, HALF)),
         vm((2, 2, 2, 2, 32, HALF)), vm((2, 2, 2, 4, 32, HALF)), vm((2, 2, 2, 2, 32, HALF)),
         vm((2, 2, 2, 16, HALF)), vm((2, 2, 2, 32, HALF)), vm((2, 2, 2, 16, HALF)),
-        vm((2, 2, 4, 32, HALF)), vm((32, DM), F32), vm((2, 2, 4, 4, 32, HALF)),
+        vm((2, 2, 4, 32, HALF)), vm((32, DM), F32), vm((4, 4, 32, DM)),
         vm((4, 4, 32, FF), F32), vm((4, 4, 32, FF)),
         pltpu.SemaphoreType.DMA((24,)),
-        pltpu.SemaphoreType.DMA((5, 10)), pltpu.SemaphoreType.DMA((5, 10)),
+        pltpu.SemaphoreType.DMA((6, 10)), pltpu.SemaphoreType.DMA((6, 10)),
         pltpu.SemaphoreType.DMA((2, 2, 2, 6)), pltpu.SemaphoreType.DMA((2, 2, 2, 6)),
         pltpu.SemaphoreType.DMA((2, 2, 2, 6)), pltpu.SemaphoreType.DMA((2, 2, 2, 6)),
     ]
     call = pl.pallas_call(
         layer_kernel,
-        out_shape=(jax.ShapeDtypeStruct((4, 4, 32, DM), BF), jax.ShapeDtypeStruct((160, SEQ), BF), jax.ShapeDtypeStruct((160, SEQ), BF)),
-        in_specs=[pl.BlockSpec(memory_space=ANY)] * 11,
-        out_specs=[pl.BlockSpec(memory_space=ANY)] * 3,
+        out_shape=(pltpu.VMEM((4, 4, 32, DM), BF), pltpu.VMEM((160, SEQ), BF), pltpu.VMEM((160, SEQ), BF)),
+        in_specs=[pl.BlockSpec(memory_space=ANY)] * 13,
+        out_specs=[pl.BlockSpec(memory_space=pltpu.VMEM)] * 3,
         scratch_shapes=scratch,
-        compiler_params=pltpu.CompilerParams(collective_id=0, has_side_effects=True, vmem_limit_bytes=62 * 1024 * 1024),
+        compiler_params=pltpu.CompilerParams(collective_id=0, has_side_effects=True, vmem_limit_bytes=56 * 1024 * 1024),
         name="layer",
     )
 
     def device_step(tokens, gain_attn, gain_mlp, w_qkv, w_rel, w_out, w_up, w_down, bias_u, bias_v, rel_table, k_cache, v_cache, positions):
-        odd = lax.axis_index("wg") % 2 == 1
-
-        def window(w):
-            return jnp.where(odd, jnp.pad(w, ((0, 0), (64, 0))), jnp.pad(w, ((0, 0), (0, 64))))
-
-        wq = window(jnp.concatenate([w_qkv.transpose(1, 2, 3, 0).reshape(480, 320), w_rel.transpose(1, 2, 0).reshape(160, 320)]))
-        wo = window(w_out.reshape(160, 320))
-        gains = window(jnp.pad(jnp.stack([gain_attn, gain_mlp]), ((0, 6), (0, 0))))
-        bias = jnp.pad(jnp.stack([bias_u.reshape(160), bias_v.reshape(160)], axis=1), ((0, 0), (0, 126)))
         out, k_new, v_new = call(
-            tokens, positions.reshape(1, SEQ), bias, gains, wq, wo, w_up, w_down.T, rel_table,
+            tokens, positions.reshape(1, SEQ), bias_u, bias_v, jnp.stack([gain_attn, gain_mlp]),
+            w_qkv.transpose(1, 2, 3, 0).reshape(480, 320), w_rel.transpose(1, 2, 0).reshape(160, 320),
+            w_out.reshape(160, 320), w_up, w_down.T, rel_table,
             k_cache.transpose(1, 2, 3, 0), v_cache.transpose(1, 2, 3, 0))
         return (out.reshape(SEQ, DM), k_new.reshape(2, HD, SEQ).transpose(2, 0, 1), v_new.reshape(2, HD, SEQ).transpose(2, 0, 1))
 

time: 156 us -> 125 us (0.80)
  Pallas kernels: 142 us -> 119 us
  local copies, waits for them, and re-layouts: 8.43 us -> 4.19 us
  other arithmetic: 4.6 us -> 0.59 us
    pallas_call x1, Pallas kernels: 142 us -> 119 us  [device_step(): call(tokens, positions.reshape(1, SEQ), bias_u, bias_v, jnp.stack([gain_a...]
    select_n x3 -> x0, other arithmetic: 3.46 us -> none  [window(): jnp.where(odd, jnp.pad(w, ((0, 0), (64, 0))), jnp.pad(w, ((0, 0), (0, 64))))]
    unnamed x7 -> x3, local copies, waits for them, and re-layouts: 4.79 us -> 2.83 us
    another operation x5 -> x2, local copies, waits for them, and re-layouts: 2.99 us -> 1.37 us  [device_step(): jnp.stack([gain_attn, gain_mlp])]
where the time goes in v3:
time: 125 us; the launch traced here: 124 us
  Pallas kernels  119 us (95%)
  local copies, waits for them, and re-layouts  4.19 us (3%)
    pallas_call x1, Pallas kernels, device_step(): call(tokens, positions.reshape(1, SEQ), bias_u, bias_v, jnp.stack([gain_a...  119 us
    unnamed x3, local copies, waits for them, and re-layouts  2.83 us

profile of v3, /device:TPU:0, one launch (start us, length us, event | category | flops | bytes accessed | tf_op | source)
XLA Modules:
  0.0 124.4 jit_solution(10558044304304244004)
XLA Ops:
  0.6 0.7 stack.9
  1.3 0.7 stack.10
  2.0 0.6 pad_maximum_fusion.gain_h
  2.6 119.0 %layer.1 = (bf16[4,4,32,2560]{3,2,1,0:T(8,128)(2,1)S(1)}, bf16[160,512]{1,0:T(8,128)(2,1)S(1)}, bf16[160,512]{1,0:T(8,128)(2,1)S(1)}) custom-call(bf16[512,2560]{1,0:T(8,128)(2,1)} %x_h.1, s32[1,512]{1,0:T(1,128)} %bitcast.27, f32[2,80]{1,0:T(2,128)} %bu_h.1, f32[2,80]{1,0:T(2,128)} %bv_h.1, f32[2,320]{1,0:T(2,128)} %pad_maximum_fusion.gain_h, ...), custom_call_target="tpu_custom_call" | custom-call | tf_op jit(solution)/shard_map/layer/pallas_call | solution.py:498
  121.6 1.5 %copy.20 = bf16[512,2560]{1,0:T(8,128)(2,1)} copy(bf16[512,2560]{1,0:T(8,128)(2,1)S(1)} %bitcast.18) | data formatting | bytes 5242880
  123.1 0.7 copy.21
  123.7 0.7 copy.22

commit v4 on v3

v4 whole, which is shorter than its diff:
```python
import jax
import jax.numpy as jnp
from jax import lax
from jax.experimental import pallas as pl
from jax.experimental.pallas import tpu as pltpu
from jax.sharding import PartitionSpec as P

NORM_EPS = 1e-6
BF = jnp.bfloat16
F32 = jnp.float32
MESH = pl.DeviceIdType.MESH
ANY = pl.ANY
SEQ, DM, HALF, HD, CL, FF = 512, 2560, 1280, 80, 32, 640
SLICE, HW = 320, 160
ME, NEXT, FAR, PREV, TAIL = range(5)
LO, HI, WHOLE = 0, 1, None
ORDER = (FAR, NEXT, PREV, ME)
NT = (((1,), (1,)), ((), ()))
NN = (((1,), (0,)), ((), ()))
TN = (((0,), (0,)), ((), ()))


def mm(a, b, dims):
    return lax.dot_general(a, b, dims, preferred_element_type=F32)


def layer_kernel(x_h, pos_h, bu_h, bv_h, ga_h, gm_h, wq_h, wr_h, wo_h, wu_h, wd_h, rt_h, k_h, v_h,
                 y_v, kn_s, vn_s,
                 x_s, pos_s, bu_s, bv_s, rt_s, wr_s, wg_s, wq_s, qp_s, wo_s, wu_s, wd_s, k_s, v_s,
                 rs_s, acc, qu_s, sc_s, ot_s, o_s, wof_s, p_s, rel_s, rcv_s, stg_s, s2_s, h_s, g_s, u_s, hid_s,
                 lsem, gsem_s, gsem_r, msem_s, rsem, asem):
    tp, wg = lax.axis_index("tp"), lax.axis_index("wg")
    z, y = tp // 4, tp % 4
    x, c = wg // 2, wg % 2

    def up1(i, d):
        return lax.rem(i + d, 4)

    def dev(dz=0, dy=0, dx=0, flip=False):
        cc = 1 - c if flip else c
        return (0, up1(z, dz) * 4 + up1(y, dy), up1(x, dx) * 2 + cc)

    xp, xm, sib = dev(dx=1), dev(dx=3), dev(flip=True)
    zp, zm, yp, ym = dev(dz=1), dev(dz=3), dev(dy=1), dev(dy=3)

    def send(src, dst, ssem, rsem, device):
        pltpu.make_async_remote_copy(src, dst, ssem, rsem, device_id=device, device_id_type=MESH).start()

    def sent(ref, ssem, rsem):
        pltpu.make_async_remote_copy(ref, ref, ssem, rsem, device_id=sib, device_id_type=MESH).wait_send()

    def arrived(dst, rsem):
        pltpu.make_async_remote_copy(dst, dst, gsem_s.at[0], rsem, device_id=sib, device_id_type=MESH).wait_recv()

    n_local = [0]

    def local(src, dst):
        cp = pltpu.make_async_copy(src, dst, lsem.at[n_local[0]])
        n_local[0] += 1
        cp.start()
        return cp

    own = 2 * x + c
    l_g = [local(ga_h, wg_s.at[own, 0, 0]), local(gm_h, wg_s.at[own, 1, 0])]
    l_q = local(wq_h, wq_s.at[own])
    l_x = local(x_h, x_s)
    l_rt = local(rt_h, rt_s)
    l_pos = local(pos_h, pos_s)
    l_bu = local(bu_h, bu_s)
    l_bv = local(bv_h, bv_s)
    l_wr = local(wr_h, wr_s)
    l_wo = local(wo_h, wo_s.at[own])
    l_wu = local(wu_h, wu_s.at[own])
    l_wd = local(wd_h, wd_s.at[own])
    l_k = local(k_h, k_s)
    l_v = local(v_h, v_s)

    barrier = pltpu.get_barrier_semaphore()
    for d in (xp, xm, sib, zp, zm, yp, ym):
        pl.semaphore_signal(barrier, inc=1, device_id=d, device_id_type=MESH)
    pl.semaphore_wait(barrier, 7)

    def slot(dx, flip=False):
        return 2 * up1(x, dx) + (1 - c if flip else c)

    class Gather:
        def __init__(self, ar, buf, rows):
            self.ar, self.buf, self.rows = ar, buf, rows

        def ref(self, s, part):
            n = self.rows // 2
            return self.buf.at[s] if part is WHOLE else self.buf.at[s, pl.ds(part * n, n)]

        def put(self, k, s, part, device):
            r = self.ref(s, part)
            send(r, r, gsem_s.at[self.ar], gsem_r.at[self.ar, k], device)

        def got(self, k, s, part):
            arrived(self.ref(s, part), gsem_r.at[self.ar, k])

        def start(self):
            o = slot(ME)
            self.put(0, o, LO, xp)
            self.put(1, o, HI, xm)
            self.put(2, o, HI, xp)
            self.put(3, o, LO, xm)
            self.put(6, o, WHOLE, sib)

        def forward(self):
            self.got(0, slot(PREV), LO)
            self.put(4, slot(PREV), LO, xp)
            self.got(1, slot(NEXT), HI)
            self.put(5, slot(NEXT), HI, xm)

        def share(self):
            self.got(2, slot(PREV), HI)
            self.put(7, slot(PREV), WHOLE, sib)
            self.got(3, slot(NEXT), LO)
            self.put(8, slot(NEXT), WHOLE, sib)

        def last(self):
            self.got(4, slot(FAR), LO)
            self.got(5, slot(FAR), HI)
            self.put(9, slot(FAR), WHOLE, sib)

        def sibling(self, dx):
            self.got({ME: 6, PREV: 7, NEXT: 8, FAR: 9}[dx], slot(dx, True), WHOLE)

        def siblings(self):
            for dx in (ME, PREV, NEXT, FAR):
                self.sibling(dx)

        def all_sent(self):
            sent(self.buf.at[pl.ds(0, 7)], gsem_s.at[self.ar], gsem_r.at[self.ar, 0])

    g_g, g_q, g_o, g_u, g_d, g_r = gathers = [Gather(i, b, r) for i, (b, r) in enumerate((
        (wg_s, 2), (wq_s, 480), (wo_s, 160), (wu_s, 320), (wd_s, 320), (qp_s, CL)))]

    for cp in l_g:
        cp.wait()
    g_g.start()
    l_q.wait()
    g_q.start()

    l_x.wait()

    def stat_rows(r, carry):
        rows = pl.ds(pl.multiple_of(r * 32, 32), 32)
        v = x_s[rows, :].astype(F32)
        ms = jnp.sum(v * v, axis=1, keepdims=True) * (1.0 / DM)
        rs_s[rows, :] = jnp.broadcast_to(lax.rsqrt(ms + NORM_EPS), (32, 128))
        return carry

    lax.fori_loop(0, 16, stat_rows, 0)
    l_rt.wait()
    l_wr.wait()
    base = pl.multiple_of(640 * x, 128)
    q_even = mm(rt_s[:, pl.ds(base, 384)][:, 0:320], wr_s[...], NT)
    q_odd = mm(rt_s[:, pl.ds(pl.multiple_of(base + 256, 128), 384)][:, 64:384], wr_s[...], NT)
    qp_s[own] = jnp.where(c == 1, q_odd, q_even)
    g_r.start()
    acc[...] = jnp.zeros_like(acc)
    u_s[...] = jnp.zeros_like(u_s)

    def qkv_pair(dx):
        xo = up1(x, dx)
        cols = pl.ds(pl.multiple_of(xo * 640, 128), 640)
        gain = jnp.concatenate([wg_s[2 * xo, 0], wg_s[2 * xo + 1, 0]], axis=1)
        n_win = (x_s[:, cols].astype(F32) * rs_s[:, 0:1] * gain).astype(BF)
        w = jnp.concatenate([wq_s[2 * xo], wq_s[2 * xo + 1]], axis=1)
        acc[...] += mm(w, n_win, NT)

    g_g.sibling(ME)
    g_q.sibling(ME)
    qkv_pair(ME)
    g_g.forward()
    g_q.forward()
    g_g.share()
    g_q.share()
    g_r.forward()
    g_r.share()
    l_wo.wait()
    g_o.start()
    g_g.last()
    for dx in (PREV, NEXT, FAR):
        g_g.sibling(dx)
        g_q.sibling(dx)
        qkv_pair(dx)
        if dx == PREV:
            g_q.last()
            g_r.last()

    kn_s[...] = acc[160:320, :].astype(BF)
    vn_s[...] = acc[320:480, :].astype(BF)
    l_pos.wait()
    l_bu.wait()
    l_bv.wait()
    g_r.siblings()
    g_o.forward()
    g_o.share()
    l_wu.wait()
    g_u.start()
    l_wd.wait()
    g_d.start()

    flip_rows = (lax.broadcasted_iota(jnp.int32, (CL, CL), 0) + lax.broadcasted_iota(jnp.int32, (CL, CL), 1)) % CL == 0
    flip_mat = jnp.where(flip_rows, 1.0, 0.0).astype(BF)
    q_rel = qp_s[0]
    for i in range(1, 8):
        q_rel = q_rel + qp_s[i]
    rel_rev = mm(flip_mat, q_rel.astype(BF), NN).astype(BF)
    diag = lax.broadcasted_iota(jnp.int32, (HD, HD), 0) == lax.broadcasted_iota(jnp.int32, (HD, HD), 1)

    def column(row):
        return jnp.sum(jnp.where(diag, row, 0.0), axis=1, keepdims=True)

    pos = pos_s[...]
    steps = lax.broadcasted_iota(jnp.int32, (CL, SEQ), 0)
    is_self = steps == pos
    l_k.wait()
    l_v.wait()

    for h in range(2):
        hr = slice(h * HD, h * HD + HD)
        q = acc[hr, :].astype(BF).astype(F32)
        q_u = (q + column(bu_s[h:h + 1, :])).astype(BF).astype(F32)
        q_v = (q + column(bv_s[h:h + 1, :])).astype(BF)
        qu_s[...] = q_u
        rel = mm(rel_rev[:, hr], q_v, NN)
        for b in range(5):
            rel = jnp.where((pos >> b) & 1 == 1, pltpu.roll(rel, 1 << b, 0), rel)
        self_score = jnp.sum(q_u * kn_s[hr, :].astype(F32), axis=0, keepdims=True)
        for lc in range(4):
            ln = slice(lc * 128, lc * 128 + 128)
            quc = qu_s[:, ln]

            def content(g, carry, h=h, ln=ln, quc=quc):
                rows = [jnp.sum(k_s[h, g * 8 + j, :, ln].astype(F32) * quc, axis=0, keepdims=True) for j in range(8)]
                sc_s[pl.ds(pl.multiple_of(g * 8, 8), 8), ln] = jnp.concatenate(rows, axis=0)
                return carry

            lax.fori_loop(0, CL // 8, content, 0)
        if h == 1:
            g_o.last()
        scores = jnp.where(is_self, self_score, sc_s[...])
        scores = jnp.where(steps <= pos, (scores + rel) * (HD ** -0.5), -1e30)
        e = jnp.exp(scores - jnp.max(scores, axis=0, keepdims=True))
        prob = (e / jnp.sum(e, axis=0, keepdims=True)).astype(BF).astype(F32)
        self_prob = jnp.sum(jnp.where(is_self, prob, 0.0), axis=0, keepdims=True)
        sc_s[...] = jnp.where(is_self, 0.0, prob)
        for lc in range(4):
            ln = slice(lc * 128, lc * 128 + 128)

            def mix(g, o, h=h, ln=ln):
                pr = sc_s[pl.ds(pl.multiple_of(g * 8, 8), 8), ln]
                for j in range(8):
                    o = o + pr[j:j + 1, :] * v_s[h, g * 8 + j, :, ln].astype(F32)
                return o

            start = self_prob[:, ln] * vn_s[hr, ln].astype(F32)
            ot_s[hr, ln] = lax.fori_loop(0, CL // 8, mix, start)

    o_s[...] = jnp.transpose(ot_s[...]).astype(BF).reshape(4, 4, 32, 160)
    g_o.siblings()
    for xo in range(4):
        wof_s[:, 640 * xo:640 * xo + 640] = jnp.concatenate([wo_s[2 * xo], wo_s[2 * xo + 1]], axis=1)

    place = ((z, y, zp, zm, yp, ym), (y, z, yp, ym, zp, zm))

    lo, hi = pl.ds(0, 16), pl.ds(16, 16)

    class Exchange:
        def __init__(self, ps, hf, e, src, fwd, bwd):
            self.src, self.fwd, self.bwd, self.sem = src, fwd, bwd, rsem.at[hf, e]
            self.ssem = msem_s.at[ps, 0, 0 if e == TAIL else 1]
            self.rel, self.rcv, self.stg = rel_s.at[ps, hf, e], rcv_s.at[ps, hf, e], stg_s.at[ps, hf, e]

        def relay(self):
            send(self.src(FAR).at[lo], self.rel.at[LO], self.ssem, self.sem.at[0], self.fwd)
            send(self.src(FAR).at[hi], self.rel.at[HI], self.ssem, self.sem.at[1], self.bwd)

        def direct(self, d):
            if d == NEXT:
                send(self.src(NEXT).at[hi], self.rcv.at[0, hi], self.ssem, self.sem.at[2], self.fwd)
            else:
                send(self.src(PREV).at[lo], self.rcv.at[1, lo], self.ssem, self.sem.at[3], self.bwd)

        def join(self):
            for part, rows, d, device in ((LO, lo, NEXT, self.fwd), (HI, hi, PREV, self.bwd)):
                arrived(self.rel.at[part], self.sem.at[part])
                both = self.src(d).at[rows][...].astype(F32) + self.rel.at[part][...].astype(F32)
                self.stg.at[part][...] = both.astype(BF)
                send(self.stg.at[part], self.rcv.at[part, rows], self.ssem, self.sem.at[4 + part], device)

        def received(self):
            for k, way, rows in ((2, 0, hi), (3, 1, lo), (4, 0, lo), (5, 1, hi)):
                arrived(self.rcv.at[way, rows], self.sem.at[k])
            return self.rcv.at[0][...].astype(F32) + self.rcv.at[1][...].astype(F32)

        def total(self):
            return self.received() + self.src(ME)[...].astype(F32)

    def reduce_scatter(ps, chunk, between):
        first, second = [], []
        for hf in range(2):
            a, b, ap, am, bp, bm = place[hf]
            first.append([Exchange(ps, hf, j, lambda d, hf=hf, a=a, b=b, j=j: p_s.at[ps, hf, up1(a, d), up1(b, j)], ap, am)
                          for j in range(4)])
            second.append(Exchange(ps, hf, TAIL, lambda d, hf=hf: s2_s.at[ps, hf, d], bp, bm))

        def directs(hf, j):
            first[hf][j].direct(NEXT)
            first[hf][j].direct(PREV)

        for hf in range(2):
            chunk(hf, up1(place[hf][0], FAR))
            for j in ORDER:
                first[hf][j].relay()
        for hf in range(2):
            chunk(hf, up1(place[hf][0], NEXT))
            chunk(hf, up1(place[hf][0], PREV))
            directs(hf, ORDER[0])
            directs(hf, ORDER[1])
        for hf in range(2):
            chunk(hf, place[hf][0])
        for t, j in enumerate(ORDER):
            for hf in range(2):
                first[hf][j].join()
                if t < 2:
                    directs(hf, ORDER[t + 2])
        between(0)
        for j in ORDER[:3]:
            for hf in range(2):
                s2_s[ps, hf, j] = first[hf][j].total().astype(BF)
                if j == FAR:
                    second[hf].relay()
                else:
                    second[hf].direct(j)
        for hf in range(2):
            second[hf].join()
        between(1)
        own_sum = [first[hf][ME].total() for hf in range(2)]
        return [own_sum[hf] + second[hf].received() for hf in range(2)]

    class Ring:
        def __init__(self, ps, hf, e, blk, fwd, bwd):
            self.blk, self.fwd, self.bwd, self.sem = blk, fwd, bwd, asem.at[hf, e]
            self.ssem = msem_s.at[ps, 1, 0 if e == TAIL else 1]

        def put(self, k, d, rows, device):
            r = self.blk(d, rows)
            send(r, r, self.ssem, self.sem.at[k], device)

        def start(self):
            self.put(0, ME, lo, self.fwd)
            self.put(1, ME, hi, self.bwd)
            self.put(2, ME, hi, self.fwd)
            self.put(3, ME, lo, self.bwd)

        def forward(self):
            arrived(self.blk(PREV, lo), self.sem.at[0])
            self.put(4, PREV, lo, self.fwd)
            arrived(self.blk(NEXT, hi), self.sem.at[1])
            self.put(5, NEXT, hi, self.bwd)

        def got(self, d):
            for k, rows in {PREV: ((2, hi),), NEXT: ((3, lo),), FAR: ((4, lo), (5, hi))}[d]:
                arrived(self.blk(d, rows), self.sem.at[k])

    def all_gather(ps, buf, consume, hook):
        inner, outer = [], []
        for hf in range(2):
            a, b, ap, am, bp, bm = place[hf]

            def block(ia, ib, rows, hf=hf):
                cols = pl.ds(hf * HALF, HALF)
                return buf.at[ia, ib, rows, cols] if hf == 0 else buf.at[ib, ia, rows, cols]

            inner.append(Ring(ps, hf, TAIL, lambda d, rows, a=a, b=b, block=block: block(a, up1(b, d), rows), bp, bm))
            outer.append([Ring(ps, hf, j, lambda d, rows, a=a, b=b, j=j, block=block: block(up1(a, d), up1(b, j), rows), ap, am)
                          for j in range(4)])
        for hf in range(2):
            inner[hf].start()
        for hf in range(2):
            outer[hf][ME].start()
        for hf in range(2):
            inner[hf].forward()
        for d in (PREV, NEXT):
            for hf in range(2):
                inner[hf].got(d)
                outer[hf][d].start()
        for hf in range(2):
            outer[hf][ME].forward()
        for hf in range(2):
            inner[hf].got(FAR)
            outer[hf][FAR].start()
        for d in (PREV, NEXT):
            for hf in range(2):
                outer[hf][d].forward()
        hook(0)
        for hf in range(2):
            consume(hf, place[hf][0])
        for hf in range(2):
            outer[hf][FAR].forward()
        for d in (PREV, NEXT, FAR):
            for hf in range(2):
                for r in outer[hf]:
                    r.got(d)
                consume(hf, up1(place[hf][0], d))
            if d == NEXT:
                hook(1)

    def out_chunk(hf, i):
        rows = (o_s[i] if hf == 0 else o_s[:, i]).reshape(128, 160)
        part = mm(rows, wof_s[:, hf * HALF:hf * HALF + HALF], NN)
        p_s[0, hf, i] = part.astype(BF).reshape(4, 32, HALF)

    def attn_between(step):
        if step == 1:
            g_u.forward()
            g_u.share()

    part = reduce_scatter(0, out_chunk, attn_between)
    mine = pl.ds(pl.multiple_of(tp * 32, 32), 32)
    for hf in range(2):
        cols = slice(hf * HALF, hf * HALF + HALF)
        h_s[:, cols] = x_s[mine, cols].astype(F32) + part[hf]
    resid = h_s[...]
    inv = lax.rsqrt(jnp.sum(resid * resid, axis=1, keepdims=True) * (1.0 / DM) + NORM_EPS)
    gain = jnp.concatenate([wg_s[i, 1] for i in range(8)], axis=1)
    g_s[z, y] = (resid * inv * gain).astype(BF)

    def mlp_hook(step):
        if step == 0:
            g_u.last()
            g_d.forward()
            g_u.siblings()
        else:
            g_d.share()
            g_d.last()

    def up_part(hf, i):
        w = wu_s[4 * hf:4 * hf + 4].reshape(HALF, FF)
        cols = slice(hf * HALF, hf * HALF + HALF)
        rows = (g_s[i, :, :, cols] if hf == 0 else g_s[:, i, :, cols]).reshape(128, HALF)
        prod = mm(rows, w, NN).reshape(4, 32, FF)
        if hf == 0:
            u_s[i] += prod
        else:
            u_s[:, i] += prod

    all_gather(0, g_s, up_part, mlp_hook)
    g_d.siblings()
    for i in range(4):
        hid_s[i] = jax.nn.gelu(u_s[i], approximate=True).astype(BF)

    def down_chunk(hf, i):
        rows = (hid_s[i] if hf == 0 else hid_s[:, i]).reshape(128, FF)
        w = wd_s[4 * hf:4 * hf + 4].reshape(HALF, FF)
        p_s[1, hf, i] = mm(rows, w, NT).astype(BF).reshape(4, 32, HALF)

    part = reduce_scatter(1, down_chunk, lambda step: None)
    y_v[z, y] = jnp.concatenate([h_s[:, 0:HALF] + part[0], h_s[:, HALF:DM] + part[1]], axis=1).astype(BF)
    all_gather(1, y_v, lambda hf, i: None, lambda step: None)
    for g in gathers:
        g.all_sent()
    for ps in range(2):
        for kind in range(2):
            sent(g_s.at[0, pl.ds(0, 3)], msem_s.at[ps, kind, 0], rsem.at[0, 0, 0])
            sent(g_s.at[pl.ds(0, 3)], msem_s.at[ps, kind, 1], rsem.at[0, 0, 0])


def solution(mesh):
    tok_axes = ("dp", "wg")
    in_specs = (P(tok_axes, None), P("wg"), P("wg"), P("wg", None, "tp", None), P("wg", "tp", None), P("tp", None, "wg"), P("wg", "tp"), P("tp", "wg"), P("tp", None), P("tp", None), P(None, None), P(tok_axes, "tp", None, None), P(tok_axes, "tp", None, None), P(tok_axes))
    out_specs = (P(tok_axes, None), P(tok_axes, "tp", None), P(tok_axes, "tp", None))

    def vm(shape, dtype=BF):
        return pltpu.VMEM(shape, dtype)

    def dma(*shape):
        return pltpu.SemaphoreType.DMA(shape)

    blocks = (2, 2, 5, 2)
    scratch = [
        vm((SEQ, DM)), vm((1, SEQ), jnp.int32), vm((2, HD), F32), vm((2, HD), F32), vm((CL, DM)), vm((HW, SLICE)),
        vm((8, 2, 1, SLICE), F32), vm((8, 3 * HW, SLICE)), vm((8, CL, HW), F32), vm((8, HW, SLICE)),
        vm((8, SLICE, FF)), vm((8, SLICE, FF)), vm((2, CL, HD, SEQ)), vm((2, CL, HD, SEQ)),
        vm((SEQ, 128), F32), vm((3 * HW, SEQ), F32), vm((HD, SEQ), F32), vm((CL, SEQ), F32),
        vm((HW, SEQ), F32), vm((4, 4, 32, HW)), vm((HW, DM)), vm((2, 2, 4, 4, 32, HALF)),
        vm(blocks + (16, HALF)), vm(blocks + (32, HALF)), vm(blocks + (16, HALF)), vm((2, 2, 4, 32, HALF)),
        vm((32, DM), F32), vm((4, 4, 32, DM)), vm((4, 4, 32, FF), F32), vm((4, 4, 32, FF)),
        dma(14), dma(6), dma(6, 10), dma(2, 2, 2), dma(2, 5, 6), dma(2, 5, 6),
    ]
    call = pl.pallas_call(
        layer_kernel,
        out_shape=(pltpu.VMEM((4, 4, 32, DM), BF), pltpu.VMEM((160, SEQ), BF), pltpu.VMEM((160, SEQ), BF)),
        in_specs=[pl.BlockSpec(memory_space=ANY)] * 14,
        out_specs=[pl.BlockSpec(memory_space=pltpu.VMEM)] * 3,
        scratch_shapes=scratch,
        compiler_params=pltpu.CompilerParams(collective_id=0, has_side_effects=True, vmem_limit_bytes=56 * 1024 * 1024),
        name="layer",
    )

    def device_step(tokens, gain_attn, gain_mlp, w_qkv, w_rel, w_out, w_up, w_down, bias_u, bias_v, rel_table, k_cache, v_cache, positions):
        out, k_new, v_new = call(
            tokens, positions.reshape(1, SEQ), bias_u, bias_v, gain_attn, gain_mlp,
            w_qkv.transpose(1, 2, 3, 0).reshape(480, 320), w_rel.transpose(1, 2, 0).reshape(160, 320),
            w_out.reshape(160, 320), w_up, w_down.T, rel_table,
            k_cache.transpose(1, 2, 3, 0), v_cache.transpose(1, 2, 3, 0))
        return (out.reshape(SEQ, DM), k_new.reshape(2, HD, SEQ).transpose(2, 0, 1), v_new.reshape(2, HD, SEQ).transpose(2, 0, 1))

    return jax.shard_map(device_step, mesh=mesh, in_specs=in_specs, out_specs=out_specs, check_vma=False)
```

time: 125 us -> 107 us (0.86)
  Pallas kernels: 119 us -> 104 us
  local copies, waits for them, and re-layouts: 4.19 us -> 2.83 us
    pallas_call x1, Pallas kernels: 119 us -> 104 us  [device_step(): call(tokens, positions.reshape(1, SEQ), bias_u, bias_v, gain_attn, gain_m...]
    another operation x2 -> x0, local copies, waits for them, and re-layouts: 1.37 us -> none  [device_step(): jnp.stack([gain_attn, gain_mlp])]
where the time goes in v4:
time: 107 us
  Pallas kernels  104 us (97%)
  local copies, waits for them, and re-layouts  2.83 us (3%)
    pallas_call x1, Pallas kernels, device_step(): call(tokens, positions.reshape(1, SEQ), bias_u, bias_v, gain_attn, gain_m...  104 us
    unnamed x3, local copies, waits for them, and re-layouts  2.83 us

profile of v4, /device:TPU:0, one launch (start us, length us, event | category | flops | bytes accessed | tf_op | source)
XLA Modules:
  0.0 107.3 jit_solution(12218722300191034127)
XLA Ops:
  0.6 103.8 %layer.1 = (bf16[4,4,32,2560]{3,2,1,0:T(8,128)(2,1)S(1)}, bf16[160,512]{1,0:T(8,128)(2,1)S(1)}, bf16[160,512]{1,0:T(8,128)(2,1)S(1)}) custom-call(bf16[512,2560]{1,0:T(8,128)(2,1)} %x_h.1, s32[1,512]{1,0:T(1,128)} %bitcast.27, f32[2,80]{1,0:T(2,128)} %bu_h.1, f32[2,80]{1,0:T(2,128)} %bv_h.1, f32[320]{0:T(512)} %ga_h.1, f32[320]{0:T(512)} %gm_h.1, ...), custom_call_target="tpu_custom_call" | custom-call | tf_op jit(solution)/shard_map/layer/pallas_call | solution.py:506
  104.4 1.5 %copy.20 = bf16[512,2560]{1,0:T(8,128)(2,1)} copy(bf16[512,2560]{1,0:T(8,128)(2,1)S(1)} %bitcast.18) | data formatting | bytes 5242880
  105.9 0.7 copy.21
  106.6 0.7 copy.22

commit v5 on v4

--- a/solution.py
+++ b/solution.py
@@ -26,8 +26,8 @@
 
 def layer_kernel(x_h, pos_h, bu_h, bv_h, ga_h, gm_h, wq_h, wr_h, wo_h, wu_h, wd_h, rt_h, k_h, v_h,
                  y_v, kn_s, vn_s,
-                 x_s, pos_s, bu_s, bv_s, rt_s, wr_s, wg_s, wq_s, qp_s, wo_s, wu_s, wd_s, k_s, v_s,
-                 rs_s, acc, qu_s, sc_s, ot_s, o_s, wof_s, p_s, rel_s, rcv_s, stg_s, s2_s, h_s, g_s, u_s, hid_s,
+                 x_s, pos_s, bu_s, bv_s, rt_s, wr_s, wqt_s, wot_s, wg_s, wq_s, qp_s, wo_s, wu_s, wd_s, k_s, v_s,
+                 rs_s, acc, qu_s, sc_s, ot_s, o_s, wof_s, p_s, rel_s, rcv_s, stg_s, s2_s, t_s, h_s, g_s, u_s, hid_s,
                  lsem, gsem_s, gsem_r, msem_s, rsem, asem):
     tp, wg = lax.axis_index("tp"), lax.axis_index("wg")
     z, y = tp // 4, tp % 4
@@ -42,6 +42,7 @@
 
     xp, xm, sib = dev(dx=1), dev(dx=3), dev(flip=True)
     zp, zm, yp, ym = dev(dz=1), dev(dz=3), dev(dy=1), dev(dy=3)
+    xf, zf, yf = dev(dx=2), dev(dz=2), dev(dy=2)
 
     def send(src, dst, ssem, rsem, device):
         pltpu.make_async_remote_copy(src, dst, ssem, rsem, device_id=device, device_id_type=MESH).start()
@@ -60,36 +61,37 @@
         cp.start()
         return cp
 
+    barrier = pltpu.get_barrier_semaphore()
+    peers = (xp, xm, xf, sib, zp, zm, zf, yp, ym, yf)
+    for d in peers:
+        pl.semaphore_signal(barrier, inc=1, device_id=d, device_id_type=MESH)
+
     own = 2 * x + c
     l_g = [local(ga_h, wg_s.at[own, 0, 0]), local(gm_h, wg_s.at[own, 1, 0])]
-    l_q = local(wq_h, wq_s.at[own])
+    l_q = local(wq_h, wqt_s)
     l_x = local(x_h, x_s)
     l_rt = local(rt_h, rt_s)
     l_pos = local(pos_h, pos_s)
     l_bu = local(bu_h, bu_s)
     l_bv = local(bv_h, bv_s)
     l_wr = local(wr_h, wr_s)
-    l_wo = local(wo_h, wo_s.at[own])
+    l_wo = local(wo_h, wot_s)
     l_wu = local(wu_h, wu_s.at[own])
     l_wd = local(wd_h, wd_s.at[own])
     l_k = local(k_h, k_s)
     l_v = local(v_h, v_s)
 
-    barrier = pltpu.get_barrier_semaphore()
-    for d in (xp, xm, sib, zp, zm, yp, ym):
-        pl.semaphore_signal(barrier, inc=1, device_id=d, device_id_type=MESH)
-    pl.semaphore_wait(barrier, 7)
-
     def slot(dx, flip=False):
         return 2 * up1(x, dx) + (1 - c if flip else c)
 
     class Gather:
-        def __init__(self, ar, buf, rows):
-            self.ar, self.buf, self.rows = ar, buf, rows
+        def __init__(self, ar, buf, rows, low):
+            self.ar, self.buf, self.rows, self.low, self.relay = ar, buf, rows, low, True
 
         def ref(self, s, part):
-            n = self.rows // 2
-            return self.buf.at[s] if part is WHOLE else self.buf.at[s, pl.ds(part * n, n)]
+            if part is WHOLE:
+                return self.buf.at[s]
+            return self.buf.at[s, pl.ds(0, self.low) if part == LO else pl.ds(self.low, self.rows - self.low)]
 
         def put(self, k, s, part, device):
             r = self.ref(s, part)
@@ -100,6 +102,9 @@
 
         def start(self):
             o = slot(ME)
+            if not self.relay:
+                self.put(4, o, LO, xf)
+                self.put(5, o, HI, xf)
             self.put(0, o, LO, xp)
             self.put(1, o, HI, xm)
             self.put(2, o, HI, xp)
@@ -108,9 +113,11 @@
 
         def forward(self):
             self.got(0, slot(PREV), LO)
-            self.put(4, slot(PREV), LO, xp)
+            if self.relay:
+                self.put(4, slot(PREV), LO, xp)
             self.got(1, slot(NEXT), HI)
-            self.put(5, slot(NEXT), HI, xm)
+            if self.relay:
+                self.put(5, slot(NEXT), HI, xm)
 
         def share(self):
             self.got(2, slot(PREV), HI)
@@ -133,15 +140,14 @@
         def all_sent(self):
             sent(self.buf.at[pl.ds(0, 7)], gsem_s.at[self.ar], gsem_r.at[self.ar, 0])
 
-    g_g, g_q, g_o, g_u, g_d, g_r = gathers = [Gather(i, b, r) for i, (b, r) in enumerate((
-        (wg_s, 2), (wq_s, 480), (wo_s, 160), (wu_s, 320), (wd_s, 320), (qp_s, CL)))]
-
-    for cp in l_g:
-        cp.wait()
-    g_g.start()
+    g_g, g_q, g_o, g_u, g_d, g_r = gathers = [Gather(i, *spec) for i, spec in enumerate((
+        (wg_s, 2, 1), (wq_s, 240, 128), (wo_s, 80, 48), (wu_s, SLICE, HW), (wd_s, SLICE, HW), (qp_s, CL, 16)))]
+    g_o.relay = False
+
     l_q.wait()
-    g_q.start()
-
+    wq_s[own] = jnp.concatenate([wqt_s[0:240, :], wqt_s[240:480, :]], axis=1)
+    l_wo.wait()
+    wo_s[own] = jnp.concatenate([wot_s[0:80, :], wot_s[80:160, :]], axis=1)
     l_x.wait()
 
     def stat_rows(r, carry):
@@ -158,17 +164,25 @@
     q_even = mm(rt_s[:, pl.ds(base, 384)][:, 0:320], wr_s[...], NT)
     q_odd = mm(rt_s[:, pl.ds(pl.multiple_of(base + 256, 128), 384)][:, 64:384], wr_s[...], NT)
     qp_s[own] = jnp.where(c == 1, q_odd, q_even)
+    for cp in l_g:
+        cp.wait()
+    pl.semaphore_wait(barrier, len(peers))
+    g_g.start()
+    g_q.start()
     g_r.start()
     acc[...] = jnp.zeros_like(acc)
     u_s[...] = jnp.zeros_like(u_s)
+
+    def unpack(even, odd):
+        halves = [jnp.concatenate([even[:, cut], odd[:, cut]], axis=1) for cut in (slice(0, SLICE), slice(SLICE, FF))]
+        return jnp.concatenate(halves, axis=0)
 
     def qkv_pair(dx):
         xo = up1(x, dx)
         cols = pl.ds(pl.multiple_of(xo * 640, 128), 640)
         gain = jnp.concatenate([wg_s[2 * xo, 0], wg_s[2 * xo + 1, 0]], axis=1)
         n_win = (x_s[:, cols].astype(F32) * rs_s[:, 0:1] * gain).astype(BF)
-        w = jnp.concatenate([wq_s[2 * xo], wq_s[2 * xo + 1]], axis=1)
-        acc[...] += mm(w, n_win, NT)
+        acc[...] += mm(unpack(wq_s[2 * xo], wq_s[2 * xo + 1]), n_win, NT)
 
     g_g.sibling(ME)
     g_q.sibling(ME)
@@ -179,7 +193,6 @@
     g_q.share()
     g_r.forward()
     g_r.share()
-    l_wo.wait()
     g_o.start()
     g_g.last()
     for dx in (PREV, NEXT, FAR):
@@ -263,16 +276,16 @@
     o_s[...] = jnp.transpose(ot_s[...]).astype(BF).reshape(4, 4, 32, 160)
     g_o.siblings()
     for xo in range(4):
-        wof_s[:, 640 * xo:640 * xo + 640] = jnp.concatenate([wo_s[2 * xo], wo_s[2 * xo + 1]], axis=1)
-
-    place = ((z, y, zp, zm, yp, ym), (y, z, yp, ym, zp, zm))
+        wof_s[:, 640 * xo:640 * xo + 640] = unpack(wo_s[2 * xo], wo_s[2 * xo + 1])
+
+    place = ((z, y, zp, zm, yp, ym, yf), (y, z, yp, ym, zp, zm, zf))
 
     lo, hi = pl.ds(0, 16), pl.ds(16, 16)
 
     class Exchange:
         def __init__(self, ps, hf, e, src, fwd, bwd):
             self.src, self.fwd, self.bwd, self.sem = src, fwd, bwd, rsem.at[hf, e]
-            self.ssem = msem_s.at[ps, 0, 0 if e == TAIL else 1]
+            self.ssem = msem_s.at[ps, 0, 1]
             self.rel, self.rcv, self.stg = rel_s.at[ps, hf, e], rcv_s.at[ps, hf, e], stg_s.at[ps, hf, e]
 
         def relay(self):
@@ -300,13 +313,26 @@
         def total(self):
             return self.received() + self.src(ME)[...].astype(F32)
 
+    class Spread:
+        def __init__(self, ps, hf, devices):
+            self.src, self.rcv, self.devices = s2_s.at[ps, hf], t_s.at[ps, hf], devices
+            self.sem, self.ssem = rsem.at[hf, TAIL], msem_s.at[ps, 0, 0]
+
+        def put(self, j):
+            send(self.src.at[j], self.rcv.at[j], self.ssem, self.sem.at[j], self.devices[j])
+
+        def received(self):
+            for j in ORDER[:3]:
+                arrived(self.rcv.at[j], self.sem.at[j])
+            return sum(self.rcv.at[j][...].astype(F32) for j in ORDER[:3])
+
     def reduce_scatter(ps, chunk, between):
         first, second = [], []
         for hf in range(2):
-            a, b, ap, am, bp, bm = place[hf]
+            a, b, ap, am, bp, bm, bf = place[hf]
             first.append([Exchange(ps, hf, j, lambda d, hf=hf, a=a, b=b, j=j: p_s.at[ps, hf, up1(a, d), up1(b, j)], ap, am)
                           for j in range(4)])
-            second.append(Exchange(ps, hf, TAIL, lambda d, hf=hf: s2_s.at[ps, hf, d], bp, bm))
+            second.append(Spread(ps, hf, {NEXT: bp, FAR: bf, PREV: bm}))
 
         def directs(hf, j):
             first[hf][j].direct(NEXT)
@@ -332,12 +358,7 @@
         for j in ORDER[:3]:
             for hf in range(2):
                 s2_s[ps, hf, j] = first[hf][j].total().astype(BF)
-                if j == FAR:
-                    second[hf].relay()
-                else:
-                    second[hf].direct(j)
-        for hf in range(2):
-            second[hf].join()
+                second[hf].put(j)
         between(1)
         own_sum = [first[hf][ME].total() for hf in range(2)]
         return [own_sum[hf] + second[hf].received() for hf in range(2)]
@@ -370,7 +391,7 @@
     def all_gather(ps, buf, consume, hook):
         inner, outer = [], []
         for hf in range(2):
-            a, b, ap, am, bp, bm = place[hf]
+            a, b, ap, am, bp, bm, _ = place[hf]
 
             def block(ia, ib, rows, hf=hf):
                 cols = pl.ds(hf * HALF, HALF)
@@ -451,14 +472,14 @@
 
     all_gather(0, g_s, up_part, mlp_hook)
     g_d.siblings()
-    for i in range(4):
-        hid_s[i] = jax.nn.gelu(u_s[i], approximate=True).astype(BF)
-
     def down_chunk(hf, i):
         rows = (hid_s[i] if hf == 0 else hid_s[:, i]).reshape(128, FF)
         w = wd_s[4 * hf:4 * hf + 4].reshape(HALF, FF)
         p_s[1, hf, i] = mm(rows, w, NT).astype(BF).reshape(4, 32, HALF)
 
+    for d in ORDER:
+        i = up1(z, d)
+        hid_s[i] = jax.nn.gelu(u_s[i], approximate=True).astype(BF)
     part = reduce_scatter(1, down_chunk, lambda step: None)
     y_v[z, y] = jnp.concatenate([h_s[:, 0:HALF] + part[0], h_s[:, HALF:DM] + part[1]], axis=1).astype(BF)
     all_gather(1, y_v, lambda hf, i: None, lambda step: None)
@@ -481,14 +502,14 @@
     def dma(*shape):
         return pltpu.SemaphoreType.DMA(shape)
 
-    blocks = (2, 2, 5, 2)
+    blocks = (2, 2, 4, 2)
     scratch = [
         vm((SEQ, DM)), vm((1, SEQ), jnp.int32), vm((2, HD), F32), vm((2, HD), F32), vm((CL, DM)), vm((HW, SLICE)),
-        vm((8, 2, 1, SLICE), F32), vm((8, 3 * HW, SLICE)), vm((8, CL, HW), F32), vm((8, HW, SLICE)),
+        vm((3 * HW, SLICE)), vm((HW, SLICE)), vm((8, 2, 1, SLICE), F32), vm((8, 240, FF)), vm((8, CL, HW), F32), vm((8, 80, FF)),
         vm((8, SLICE, FF)), vm((8, SLICE, FF)), vm((2, CL, HD, SEQ)), vm((2, CL, HD, SEQ)),
         vm((SEQ, 128), F32), vm((3 * HW, SEQ), F32), vm((HD, SEQ), F32), vm((CL, SEQ), F32),
         vm((HW, SEQ), F32), vm((4, 4, 32, HW)), vm((HW, DM)), vm((2, 2, 4, 4, 32, HALF)),
-        vm(blocks + (16, HALF)), vm(blocks + (32, HALF)), vm(blocks + (16, HALF)), vm((2, 2, 4, 32, HALF)),
+        vm(blocks + (16, HALF)), vm(blocks + (32, HALF)), vm(blocks + (16, HALF)), vm((2, 2, 4, 32, HALF)), vm((2, 2, 4, 32, HALF)),
         vm((32, DM), F32), vm((4, 4, 32, DM)), vm((4, 4, 32, FF), F32), vm((4, 4, 32, FF)),
         dma(14), dma(6), dma(6, 10), dma(2, 2, 2), dma(2, 5, 6), dma(2, 5, 6),
     ]

time: 107 us -> 107 us (level)
  no operation moved by 1% of the time
where the time goes in v5:
time: 107 us
  Pallas kernels  104 us (97%)
  local copies, waits for them, and re-layouts  2.83 us (3%)
    pallas_call x1, Pallas kernels, device_step(): call(tokens, positions.reshape(1, SEQ), bias_u, bias_v, gain_attn, gain_m...  104 us
    unnamed x3, local copies, waits for them, and re-layouts  2.83 us

profile of v5, /device:TPU:0, one launch (start us, length us, event | category | flops | bytes accessed | tf_op | source)
XLA Modules:
  0.0 107.3 jit_solution(10389858193697701857)
XLA Ops:
  0.6 103.8 %layer.1 = (bf16[4,4,32,2560]{3,2,1,0:T(8,128)(2,1)S(1)}, bf16[160,512]{1,0:T(8,128)(2,1)S(1)}, bf16[160,512]{1,0:T(8,128)(2,1)S(1)}) custom-call(bf16[512,2560]{1,0:T(8,128)(2,1)} %x_h.1, s32[1,512]{1,0:T(1,128)} %bitcast.27, f32[2,80]{1,0:T(2,128)} %bu_h.1, f32[2,80]{1,0:T(2,128)} %bv_h.1, f32[320]{0:T(512)} %ga_h.1, f32[320]{0:T(512)} %gm_h.1, ...), custom_call_target="tpu_custom_call" | custom-call | tf_op jit(solution)/shard_map/layer/pallas_call | solution.py:527
  104.5 1.5 %copy.20 = bf16[512,2560]{1,0:T(8,128)(2,1)} copy(bf16[512,2560]{1,0:T(8,128)(2,1)S(1)} %bitcast.18) | data formatting | bytes 5242880
  106.0 0.7 copy.21
  106.6 0.7 copy.22

commit v6 on v5

--- a/solution.py
+++ b/solution.py
@@ -27,7 +27,7 @@
 def layer_kernel(x_h, pos_h, bu_h, bv_h, ga_h, gm_h, wq_h, wr_h, wo_h, wu_h, wd_h, rt_h, k_h, v_h,
                  y_v, kn_s, vn_s,
                  x_s, pos_s, bu_s, bv_s, rt_s, wr_s, wqt_s, wot_s, wg_s, wq_s, qp_s, wo_s, wu_s, wd_s, k_s, v_s,
-                 rs_s, acc, qu_s, sc_s, ot_s, o_s, wof_s, p_s, rel_s, rcv_s, stg_s, s2_s, t_s, h_s, g_s, u_s, hid_s,
+                 rs_s, acc, qu_s, sc_s, ot_s, o_s, wof_s, p_s, rel_s, rcv_s, stg_s, s2_s, t_s, h_s, g_s, u_s, hid_s, n_s,
                  lsem, gsem_s, gsem_r, msem_s, rsem, asem):
     tp, wg = lax.axis_index("tp"), lax.axis_index("wg")
     z, y = tp // 4, tp % 4
@@ -180,12 +180,12 @@
     def qkv_pair(dx):
         xo = up1(x, dx)
         cols = pl.ds(pl.multiple_of(xo * 640, 128), 640)
+        g_g.sibling(dx)
         gain = jnp.concatenate([wg_s[2 * xo, 0], wg_s[2 * xo + 1, 0]], axis=1)
-        n_win = (x_s[:, cols].astype(F32) * rs_s[:, 0:1] * gain).astype(BF)
-        acc[...] += mm(unpack(wq_s[2 * xo], wq_s[2 * xo + 1]), n_win, NT)
-
-    g_g.sibling(ME)
-    g_q.sibling(ME)
+        n_s[...] = (x_s[:, cols].astype(F32) * rs_s[:, 0:1] * gain).astype(BF)
+        g_q.sibling(dx)
+        acc[...] += mm(unpack(wq_s[2 * xo], wq_s[2 * xo + 1]), n_s[...], NT)
+
     qkv_pair(ME)
     g_g.forward()
     g_q.forward()
@@ -196,8 +196,6 @@
     g_o.start()
     g_g.last()
     for dx in (PREV, NEXT, FAR):
-        g_g.sibling(dx)
-        g_q.sibling(dx)
         qkv_pair(dx)
         if dx == PREV:
             g_q.last()
@@ -354,12 +352,12 @@
                 first[hf][j].join()
                 if t < 2:
                     directs(hf, ORDER[t + 2])
-        between(0)
         for j in ORDER[:3]:
             for hf in range(2):
                 s2_s[ps, hf, j] = first[hf][j].total().astype(BF)
                 second[hf].put(j)
-        between(1)
+            if j == FAR:
+                between()
         own_sum = [first[hf][ME].total() for hf in range(2)]
         return [own_sum[hf] + second[hf].received() for hf in range(2)]
 
@@ -410,6 +408,7 @@
             for hf in range(2):
                 inner[hf].got(d)
                 outer[hf][d].start()
+        hook(0)
         for hf in range(2):
             outer[hf][ME].forward()
         for hf in range(2):
@@ -418,7 +417,7 @@
         for d in (PREV, NEXT):
             for hf in range(2):
                 outer[hf][d].forward()
-        hook(0)
+        hook(1)
         for hf in range(2):
             consume(hf, place[hf][0])
         for hf in range(2):
@@ -429,17 +428,16 @@
                     r.got(d)
                 consume(hf, up1(place[hf][0], d))
             if d == NEXT:
-                hook(1)
+                hook(2)
 
     def out_chunk(hf, i):
         rows = (o_s[i] if hf == 0 else o_s[:, i]).reshape(128, 160)
         part = mm(rows, wof_s[:, hf * HALF:hf * HALF + HALF], NN)
         p_s[0, hf, i] = part.astype(BF).reshape(4, 32, HALF)
 
-    def attn_between(step):
-        if step == 1:
-            g_u.forward()
-            g_u.share()
+    def attn_between():
+        g_u.forward()
+        g_u.share()
 
     part = reduce_scatter(0, out_chunk, attn_between)
     mine = pl.ds(pl.multiple_of(tp * 32, 32), 32)
@@ -455,9 +453,10 @@
         if step == 0:
             g_u.last()
             g_d.forward()
+        elif step == 1:
+            g_d.share()
             g_u.siblings()
         else:
-            g_d.share()
             g_d.last()
 
     def up_part(hf, i):
@@ -472,15 +471,18 @@
 
     all_gather(0, g_s, up_part, mlp_hook)
     g_d.siblings()
+    todo = [FAR], [NEXT, PREV, ME], [], [], [], [], [], []
+    calls = iter(todo)
+
     def down_chunk(hf, i):
+        for d in next(calls):
+            k = up1(z, d)
+            hid_s[k] = jax.nn.gelu(u_s[k], approximate=True).astype(BF)
         rows = (hid_s[i] if hf == 0 else hid_s[:, i]).reshape(128, FF)
         w = wd_s[4 * hf:4 * hf + 4].reshape(HALF, FF)
         p_s[1, hf, i] = mm(rows, w, NT).astype(BF).reshape(4, 32, HALF)
 
-    for d in ORDER:
-        i = up1(z, d)
-        hid_s[i] = jax.nn.gelu(u_s[i], approximate=True).astype(BF)
-    part = reduce_scatter(1, down_chunk, lambda step: None)
+    part = reduce_scatter(1, down_chunk, lambda: None)
     y_v[z, y] = jnp.concatenate([h_s[:, 0:HALF] + part[0], h_s[:, HALF:DM] + part[1]], axis=1).astype(BF)
     all_gather(1, y_v, lambda hf, i: None, lambda step: None)
     for g in gathers:
@@ -491,6 +493,14 @@
             sent(g_s.at[pl.ds(0, 3)], msem_s.at[ps, kind, 1], rsem.at[0, 0, 0])
 
 
+def result_kernel(y_v, k_v, v_v, y_h, k_h, v_h, sem):
+    copies = [pltpu.make_async_copy(src, dst, sem.at[i]) for i, (src, dst) in enumerate(((y_v, y_h), (k_v, k_h), (v_v, v_h)))]
+    for cp in copies:
+        cp.start()
+    for cp in copies:
+        cp.wait()
+
+
 def solution(mesh):
     tok_axes = ("dp", "wg")
     in_specs = (P(tok_axes, None), P("wg"), P("wg"), P("wg", None, "tp", None), P("wg", "tp", None), P("tp", None, "wg"), P("wg", "tp"), P("tp", "wg"), P("tp", None), P("tp", None), P(None, None), P(tok_axes, "tp", None, None), P(tok_axes, "tp", None, None), P(tok_axes))
@@ -510,12 +520,12 @@
         vm((SEQ, 128), F32), vm((3 * HW, SEQ), F32), vm((HD, SEQ), F32), vm((CL, SEQ), F32),
         vm((HW, SEQ), F32), vm((4, 4, 32, HW)), vm((HW, DM)), vm((2, 2, 4, 4, 32, HALF)),
         vm(blocks + (16, HALF)), vm(blocks + (32, HALF)), vm(blocks + (16, HALF)), vm((2, 2, 4, 32, HALF)), vm((2, 2, 4, 32, HALF)),
-        vm((32, DM), F32), vm((4, 4, 32, DM)), vm((4, 4, 32, FF), F32), vm((4, 4, 32, FF)),
+        vm((32, DM), F32), vm((4, 4, 32, DM)), vm((4, 4, 32, FF), F32), vm((4, 4, 32, FF)), vm((SEQ, FF)),
         dma(14), dma(6), dma(6, 10), dma(2, 2, 2), dma(2, 5, 6), dma(2, 5, 6),
     ]
     call = pl.pallas_call(
         layer_kernel,
-        out_shape=(pltpu.VMEM((4, 4, 32, DM), BF), pltpu.VMEM((160, SEQ), BF), pltpu.VMEM((160, SEQ), BF)),
+        out_shape=[vm((4, 4, 32, DM)), vm((HW, SEQ)), vm((HW, SEQ))],
         in_specs=[pl.BlockSpec(memory_space=ANY)] * 14,
         out_specs=[pl.BlockSpec(memory_space=pltpu.VMEM)] * 3,
         scratch_shapes=scratch,
@@ -523,12 +533,23 @@
         name="layer",
     )
 
+    shapes = ((4, 4, 32, DM), (HW, SEQ), (HW, SEQ))
+    write = pl.pallas_call(
+        result_kernel,
+        out_shape=[jax.ShapeDtypeStruct(shape, BF) for shape in shapes],
+        in_specs=[pl.BlockSpec(memory_space=pltpu.VMEM)] * 3,
+        out_specs=[pl.BlockSpec(memory_space=ANY)] * 3,
+        scratch_shapes=[dma(3)],
+        compiler_params=pltpu.CompilerParams(vmem_limit_bytes=1 << 20),
+        name="results",
+    )
+
     def device_step(tokens, gain_attn, gain_mlp, w_qkv, w_rel, w_out, w_up, w_down, bias_u, bias_v, rel_table, k_cache, v_cache, positions):
-        out, k_new, v_new = call(
+        out, k_new, v_new = write(*call(
             tokens, positions.reshape(1, SEQ), bias_u, bias_v, gain_attn, gain_mlp,
             w_qkv.transpose(1, 2, 3, 0).reshape(480, 320), w_rel.transpose(1, 2, 0).reshape(160, 320),
             w_out.reshape(160, 320), w_up, w_down.T, rel_table,
-            k_cache.transpose(1, 2, 3, 0), v_cache.transpose(1, 2, 3, 0))
+            k_cache.transpose(1, 2, 3, 0), v_cache.transpose(1, 2, 3, 0)))
         return (out.reshape(SEQ, DM), k_new.reshape(2, HD, SEQ).transpose(2, 0, 1), v_new.reshape(2, HD, SEQ).transpose(2, 0, 1))
 
     return jax.shard_map(device_step, mesh=mesh, in_specs=in_specs, out_specs=out_specs, check_vma=False)

time: 107 us -> 106 us (level)
  local copies, waits for them, and re-layouts: 2.83 us -> 0 us
    unnamed x3 -> x0, local copies, waits for them, and re-layouts: 2.83 us -> none
    pallas_call x0 -> x1, Pallas kernels: none -> 1.61 us  [device_step(): write(*call(tokens, positions.reshape(1, SEQ), bias_u, bias_v, gain_attn,...]
where the time goes in v6:
time: 106 us
  Pallas kernels  105 us (99%)
    pallas_call x1, Pallas kernels, device_step(): call(tokens, positions.reshape(1, SEQ), bias_u, bias_v, gain_attn, gain_m...  104 us

profile of v6, /device:TPU:0, one launch (start us, length us, event | category | flops | bytes accessed | tf_op | source)
XLA Modules:
  0.0 106.2 jit_solution(7479633573645141278)
XLA Ops:
  0.6 103.8 %layer.1 = (bf16[4,4,32,2560]{3,2,1,0:T(8,128)(2,1)S(1)}, bf16[160,512]{1,0:T(8,128)(2,1)S(1)}, bf16[160,512]{1,0:T(8,128)(2,1)S(1)}) custom-call(bf16[512,2560]{1,0:T(8,128)(2,1)} %x_h.1, s32[1,512]{1,0:T(1,128)} %bitcast.24, f32[2,80]{1,0:T(2,128)} %bu_h.1, f32[2,80]{1,0:T(2,128)} %bv_h.1, f32[320]{0:T(512)} %ga_h.1, f32[320]{0:T(512)} %gm_h.1, ...), custom_call_target="tpu_custom_call" | custom-call | tf_op jit(solution)/shard_map/layer/pallas_call | solution.py:548
  104.5 1.6 %results.1 = (bf16[4,4,32,2560]{3,2,1,0:T(8,128)(2,1)}, bf16[160,512]{1,0:T(8,128)(2,1)}, bf16[160,512]{1,0:T(8,128)(2,1)}) custom-call(bf16[4,4,32,2560]{3,2,1,0:T(8,128)(2,1)S(1)} %get-tuple-element.9.y_v, bf16[160,512]{1,0:T(8,128)(2,1)S(1)} %get-tuple-element.10.k_v, bf16[160,512]{1,0:T(8,128)(2,1)S(1)} %get-tuple-element.11.v_v), custom_call_target="tpu_custom_call" | custom-call | tf_op jit(solution)/shard_map/results/pallas_call | solution.py:548

commit v7 on v6

--- a/solution.py
+++ b/solution.py
@@ -11,9 +11,10 @@
 MESH = pl.DeviceIdType.MESH
 ANY = pl.ANY
 SEQ, DM, HALF, HD, CL, FF = 512, 2560, 1280, 80, 32, 640
-SLICE, HW = 320, 160
+SLICE, HW, QK = 320, 160, 320
 ME, NEXT, FAR, PREV, TAIL = range(5)
 LO, HI, WHOLE = 0, 1, None
+BOTH = range(2)
 ORDER = (FAR, NEXT, PREV, ME)
 NT = (((1,), (1,)), ((), ()))
 NN = (((1,), (0,)), ((), ()))
@@ -26,8 +27,8 @@
 
 def layer_kernel(x_h, pos_h, bu_h, bv_h, ga_h, gm_h, wq_h, wr_h, wo_h, wu_h, wd_h, rt_h, k_h, v_h,
                  y_v, kn_s, vn_s,
-                 x_s, pos_s, bu_s, bv_s, rt_s, wr_s, wqt_s, wot_s, wg_s, wq_s, qp_s, wo_s, wu_s, wd_s, k_s, v_s,
-                 rs_s, acc, qu_s, sc_s, ot_s, o_s, wof_s, p_s, rel_s, rcv_s, stg_s, s2_s, t_s, h_s, g_s, u_s, hid_s, n_s,
+                 x_s, pos_s, bu_s, bv_s, rt_s, wr_s, wqt_s, wot_s, wg_s, wk_s, wv_s, qp_s, wo_s, wu_s, wd_s, k_s, v_s,
+                 rs_s, acc, qu_s, sc_s, sp_s, ot_s, o_s, wof_s, p_s, rel_s, rcv_s, stg_s, s2_s, t_s, h_s, g_s, u_s, hid_s, n_s,
                  lsem, gsem_s, gsem_r, msem_s, rsem, asem):
     tp, wg = lax.axis_index("tp"), lax.axis_index("wg")
     z, y = tp // 4, tp % 4
@@ -140,12 +141,13 @@
         def all_sent(self):
             sent(self.buf.at[pl.ds(0, 7)], gsem_s.at[self.ar], gsem_r.at[self.ar, 0])
 
-    g_g, g_q, g_o, g_u, g_d, g_r = gathers = [Gather(i, *spec) for i, spec in enumerate((
-        (wg_s, 2, 1), (wq_s, 240, 128), (wo_s, 80, 48), (wu_s, SLICE, HW), (wd_s, SLICE, HW), (qp_s, CL, 16)))]
-    g_o.relay = False
+    g_g, g_k, g_v, g_o, g_u, g_d, g_r = gathers = [Gather(i, *spec) for i, spec in enumerate((
+        (wg_s, 2, 1), (wk_s, HW, 80), (wv_s, 80, 48), (wo_s, 80, 48), (wu_s, SLICE, HW), (wd_s, SLICE, HW), (qp_s, CL, 16)))]
+    g_v.relay = g_o.relay = False
 
     l_q.wait()
-    wq_s[own] = jnp.concatenate([wqt_s[0:240, :], wqt_s[240:480, :]], axis=1)
+    wk_s[own] = jnp.concatenate([wqt_s[0:HW, :], wqt_s[HW:QK, :]], axis=1)
+    wv_s[own] = jnp.concatenate([wqt_s[QK:400, :], wqt_s[400:480, :]], axis=1)
     l_wo.wait()
     wo_s[own] = jnp.concatenate([wot_s[0:80, :], wot_s[80:160, :]], axis=1)
     l_x.wait()
@@ -168,7 +170,7 @@
         cp.wait()
     pl.semaphore_wait(barrier, len(peers))
     g_g.start()
-    g_q.start()
+    g_k.start()
     g_r.start()
     acc[...] = jnp.zeros_like(acc)
     u_s[...] = jnp.zeros_like(u_s)
@@ -177,42 +179,48 @@
         halves = [jnp.concatenate([even[:, cut], odd[:, cut]], axis=1) for cut in (slice(0, SLICE), slice(SLICE, FF))]
         return jnp.concatenate(halves, axis=0)
 
-    def qkv_pair(dx):
+    def norm_cols(dx):
         xo = up1(x, dx)
         cols = pl.ds(pl.multiple_of(xo * 640, 128), 640)
         g_g.sibling(dx)
         gain = jnp.concatenate([wg_s[2 * xo, 0], wg_s[2 * xo + 1, 0]], axis=1)
-        n_s[...] = (x_s[:, cols].astype(F32) * rs_s[:, 0:1] * gain).astype(BF)
-        g_q.sibling(dx)
-        acc[...] += mm(unpack(wq_s[2 * xo], wq_s[2 * xo + 1]), n_s[...], NT)
-
-    qkv_pair(ME)
+        n_s[dx] = (x_s[:, cols].astype(F32) * rs_s[:, 0:1] * gain).astype(BF)
+
+    def pair(g, buf, rows, dx):
+        xo = up1(x, dx)
+        g.sibling(dx)
+        acc[rows, :] += mm(unpack(buf[2 * xo], buf[2 * xo + 1]), n_s[dx], NT)
+
+    qk_rows, v_rows = slice(0, QK), slice(QK, None)
+    norm_cols(ME)
+    pair(g_k, wk_s, qk_rows, ME)
     g_g.forward()
-    g_q.forward()
+    g_k.forward()
+    g_r.forward()
+    g_v.start()
+    g_o.start()
     g_g.share()
-    g_q.share()
-    g_r.forward()
+    g_k.share()
     g_r.share()
-    g_o.start()
+    l_wu.wait()
+    g_u.start()
+    l_wd.wait()
+    g_d.start()
     g_g.last()
     for dx in (PREV, NEXT, FAR):
-        qkv_pair(dx)
-        if dx == PREV:
-            g_q.last()
-            g_r.last()
-
-    kn_s[...] = acc[160:320, :].astype(BF)
-    vn_s[...] = acc[320:480, :].astype(BF)
+        norm_cols(dx)
+    pair(g_k, wk_s, qk_rows, PREV)
+    g_k.last()
+    g_r.last()
+    pair(g_k, wk_s, qk_rows, NEXT)
+    pair(g_v, wv_s, v_rows, ME)
+    pair(g_k, wk_s, qk_rows, FAR)
+
+    kn_s[...] = acc[HW:QK, :].astype(BF)
     l_pos.wait()
     l_bu.wait()
     l_bv.wait()
     g_r.siblings()
-    g_o.forward()
-    g_o.share()
-    l_wu.wait()
-    g_u.start()
-    l_wd.wait()
-    g_d.start()
 
     flip_rows = (lax.broadcasted_iota(jnp.int32, (CL, CL), 0) + lax.broadcasted_iota(jnp.int32, (CL, CL), 1)) % CL == 0
     flip_mat = jnp.where(flip_rows, 1.0, 0.0).astype(BF)
@@ -225,13 +233,13 @@
     def column(row):
         return jnp.sum(jnp.where(diag, row, 0.0), axis=1, keepdims=True)
 
+    lanes = [slice(first, first + 128) for first in range(0, SEQ, 128)]
     pos = pos_s[...]
     steps = lax.broadcasted_iota(jnp.int32, (CL, SEQ), 0)
     is_self = steps == pos
     l_k.wait()
-    l_v.wait()
-
-    for h in range(2):
+
+    for h in BOTH:
         hr = slice(h * HD, h * HD + HD)
         q = acc[hr, :].astype(BF).astype(F32)
         q_u = (q + column(bu_s[h:h + 1, :])).astype(BF).astype(F32)
@@ -241,37 +249,47 @@
         for b in range(5):
             rel = jnp.where((pos >> b) & 1 == 1, pltpu.roll(rel, 1 << b, 0), rel)
         self_score = jnp.sum(q_u * kn_s[hr, :].astype(F32), axis=0, keepdims=True)
-        for lc in range(4):
-            ln = slice(lc * 128, lc * 128 + 128)
+        for ln in lanes:
             quc = qu_s[:, ln]
 
             def content(g, carry, h=h, ln=ln, quc=quc):
                 rows = [jnp.sum(k_s[h, g * 8 + j, :, ln].astype(F32) * quc, axis=0, keepdims=True) for j in range(8)]
-                sc_s[pl.ds(pl.multiple_of(g * 8, 8), 8), ln] = jnp.concatenate(rows, axis=0)
+                sc_s[h, pl.ds(pl.multiple_of(g * 8, 8), 8), ln] = jnp.concatenate(rows, axis=0)
                 return carry
 
             lax.fori_loop(0, CL // 8, content, 0)
-        if h == 1:
-            g_o.last()
-        scores = jnp.where(is_self, self_score, sc_s[...])
+        scores = jnp.where(is_self, self_score, sc_s[h])
         scores = jnp.where(steps <= pos, (scores + rel) * (HD ** -0.5), -1e30)
         e = jnp.exp(scores - jnp.max(scores, axis=0, keepdims=True))
         prob = (e / jnp.sum(e, axis=0, keepdims=True)).astype(BF).astype(F32)
-        self_prob = jnp.sum(jnp.where(is_self, prob, 0.0), axis=0, keepdims=True)
-        sc_s[...] = jnp.where(is_self, 0.0, prob)
-        for lc in range(4):
-            ln = slice(lc * 128, lc * 128 + 128)
+        sp_s[h] = jnp.sum(jnp.where(is_self, prob, 0.0), axis=0, keepdims=True)
+        sc_s[h] = jnp.where(is_self, 0.0, prob)
+        if h == 0:
+            g_v.forward()
+            g_v.share()
+            g_v.last()
+
+    for dx in (PREV, NEXT, FAR):
+        pair(g_v, wv_s, v_rows, dx)
+    vn_s[...] = acc[v_rows, :].astype(BF)
+    l_v.wait()
+    for h in BOTH:
+        hr = slice(h * HD, h * HD + HD)
+        for ln in lanes:
 
             def mix(g, o, h=h, ln=ln):
-                pr = sc_s[pl.ds(pl.multiple_of(g * 8, 8), 8), ln]
+                pr = sc_s[h, pl.ds(pl.multiple_of(g * 8, 8), 8), ln]
                 for j in range(8):
                     o = o + pr[j:j + 1, :] * v_s[h, g * 8 + j, :, ln].astype(F32)
                 return o
 
-            start = self_prob[:, ln] * vn_s[hr, ln].astype(F32)
+            start = sp_s[h, :, ln] * vn_s[hr, ln].astype(F32)
             ot_s[hr, ln] = lax.fori_loop(0, CL // 8, mix, start)
 
     o_s[...] = jnp.transpose(ot_s[...]).astype(BF).reshape(4, 4, 32, 160)
+    g_o.forward()
+    g_o.share()
+    g_o.last()
     g_o.siblings()
     for xo in range(4):
         wof_s[:, 640 * xo:640 * xo + 640] = unpack(wo_s[2 * xo], wo_s[2 * xo + 1])
@@ -326,7 +344,7 @@
 
     def reduce_scatter(ps, chunk, between):
         first, second = [], []
-        for hf in range(2):
+        for hf in BOTH:
             a, b, ap, am, bp, bm, bf = place[hf]
             first.append([Exchange(ps, hf, j, lambda d, hf=hf, a=a, b=b, j=j: p_s.at[ps, hf, up1(a, d), up1(b, j)], ap, am)
                           for j in range(4)])
@@ -336,30 +354,30 @@
             first[hf][j].direct(NEXT)
             first[hf][j].direct(PREV)
 
-        for hf in range(2):
+        for hf in BOTH:
             chunk(hf, up1(place[hf][0], FAR))
             for j in ORDER:
                 first[hf][j].relay()
-        for hf in range(2):
+        for hf in BOTH:
             chunk(hf, up1(place[hf][0], NEXT))
             chunk(hf, up1(place[hf][0], PREV))
             directs(hf, ORDER[0])
             directs(hf, ORDER[1])
-        for hf in range(2):
+        for hf in BOTH:
             chunk(hf, place[hf][0])
         for t, j in enumerate(ORDER):
-            for hf in range(2):
+            for hf in BOTH:
                 first[hf][j].join()
                 if t < 2:
                     directs(hf, ORDER[t + 2])
         for j in ORDER[:3]:
-            for hf in range(2):
+            for hf in BOTH:
                 s2_s[ps, hf, j] = first[hf][j].total().astype(BF)
                 second[hf].put(j)
             if j == FAR:
                 between()
-        own_sum = [first[hf][ME].total() for hf in range(2)]
-        return [own_sum[hf] + second[hf].received() for hf in range(2)]
+        own_sum = [first[hf][ME].total() for hf in BOTH]
+        return [own_sum[hf] + second[hf].received() for hf in BOTH]
 
     class Ring:
         def __init__(self, ps, hf, e, blk, fwd, bwd):
@@ -388,7 +406,7 @@
 
     def all_gather(ps, buf, consume, hook):
         inner, outer = [], []
-        for hf in range(2):
+        for hf in BOTH:
             a, b, ap, am, bp, bm, _ = place[hf]
 
             def block(ia, ib, rows, hf=hf):
@@ -398,32 +416,32 @@
             inner.append(Ring(ps, hf, TAIL, lambda d, rows, a=a, b=b, block=block: block(a, up1(b, d), rows), bp, bm))
             outer.append([Ring(ps, hf, j, lambda d, rows, a=a, b=b, j=j, block=block: block(up1(a, d), up1(b, j), rows), ap, am)
                           for j in range(4)])
-        for hf in range(2):
+        for hf in BOTH:
             inner[hf].start()
-        for hf in range(2):
+        for hf in BOTH:
             outer[hf][ME].start()
-        for hf in range(2):
+        for hf in BOTH:
             inner[hf].forward()
         for d in (PREV, NEXT):
-            for hf in range(2):
+            for hf in BOTH:
                 inner[hf].got(d)
                 outer[hf][d].start()
         hook(0)
-        for hf in range(2):
+        for hf in BOTH:
             outer[hf][ME].forward()
-        for hf in range(2):
+        for hf in BOTH:
             inner[hf].got(FAR)
             outer[hf][FAR].start()
         for d in (PREV, NEXT):
-            for hf in range(2):
+            for hf in BOTH:
                 outer[hf][d].forward()
         hook(1)
-        for hf in range(2):
+        for hf in BOTH:
             consume(hf, place[hf][0])
-        for hf in range(2):
+        for hf in BOTH:
             outer[hf][FAR].forward()
         for d in (PREV, NEXT, FAR):
-            for hf in range(2):
+            for hf in BOTH:
                 for r in outer[hf]:
                     r.got(d)
                 consume(hf, up1(place[hf][0], d))
@@ -441,7 +459,7 @@
 
     part = reduce_scatter(0, out_chunk, attn_between)
     mine = pl.ds(pl.multiple_of(tp * 32, 32), 32)
-    for hf in range(2):
+    for hf in BOTH:
         cols = slice(hf * HALF, hf * HALF + HALF)
         h_s[:, cols] = x_s[mine, cols].astype(F32) + part[hf]
     resid = h_s[...]
@@ -487,8 +505,8 @@
     all_gather(1, y_v, lambda hf, i: None, lambda step: None)
     for g in gathers:
         g.all_sent()
-    for ps in range(2):
-        for kind in range(2):
+    for ps in BOTH:
+        for kind in BOTH:
             sent(g_s.at[0, pl.ds(0, 3)], msem_s.at[ps, kind, 0], rsem.at[0, 0, 0])
             sent(g_s.at[pl.ds(0, 3)], msem_s.at[ps, kind, 1], rsem.at[0, 0, 0])
 
@@ -515,13 +533,13 @@
     blocks = (2, 2, 4, 2)
     scratch = [
         vm((SEQ, DM)), vm((1, SEQ), jnp.int32), vm((2, HD), F32), vm((2, HD), F32), vm((CL, DM)), vm((HW, SLICE)),
-        vm((3 * HW, SLICE)), vm((HW, SLICE)), vm((8, 2, 1, SLICE), F32), vm((8, 240, FF)), vm((8, CL, HW), F32), vm((8, 80, FF)),
+        vm((3 * HW, SLICE)), vm((HW, SLICE)), vm((8, 2, 1, SLICE), F32), vm((8, HW, FF)), vm((8, 80, FF)), vm((8, CL, HW), F32), vm((8, 80, FF)),
         vm((8, SLICE, FF)), vm((8, SLICE, FF)), vm((2, CL, HD, SEQ)), vm((2, CL, HD, SEQ)),
-        vm((SEQ, 128), F32), vm((3 * HW, SEQ), F32), vm((HD, SEQ), F32), vm((CL, SEQ), F32),
+        vm((SEQ, 128), F32), vm((3 * HW, SEQ), F32), vm((HD, SEQ), F32), vm((2, CL, SEQ), F32), vm((2, 1, SEQ), F32),
         vm((HW, SEQ), F32), vm((4, 4, 32, HW)), vm((HW, DM)), vm((2, 2, 4, 4, 32, HALF)),
         vm(blocks + (16, HALF)), vm(blocks + (32, HALF)), vm(blocks + (16, HALF)), vm((2, 2, 4, 32, HALF)), vm((2, 2, 4, 32, HALF)),
-        vm((32, DM), F32), vm((4, 4, 32, DM)), vm((4, 4, 32, FF), F32), vm((4, 4, 32, FF)), vm((SEQ, FF)),
-        dma(14), dma(6), dma(6, 10), dma(2, 2, 2), dma(2, 5, 6), dma(2, 5, 6),
+        vm((32, DM), F32), vm((4, 4, 32, DM)), vm((4, 4, 32, FF), F32), vm((4, 4, 32, FF)), vm((4, SEQ, FF)),
+        dma(14), dma(7), dma(7, 10), dma(2, 2, 2), dma(2, 5, 6), dma(2, 5, 6),
     ]
     call = pl.pallas_call(
         layer_kernel,

time: 106 us -> 106 us (level)
  no operation moved by 1% of the time
where the time goes in v7:
time: 106 us
  Pallas kernels  105 us (99%)
    pallas_call x1, Pallas kernels, device_step(): call(tokens, positions.reshape(1, SEQ), bias_u, bias_v, gain_attn, gain_m...  103 us

profile of v7, /device:TPU:0, one launch (start us, length us, event | category | flops | bytes accessed | tf_op | source)
XLA Modules:
  0.0 105.8 jit_solution(1291643072129868240)
XLA Ops:
  0.6 103.4 %layer.1 = (bf16[4,4,32,2560]{3,2,1,0:T(8,128)(2,1)S(1)}, bf16[160,512]{1,0:T(8,128)(2,1)S(1)}, bf16[160,512]{1,0:T(8,128)(2,1)S(1)}) custom-call(bf16[512,2560]{1,0:T(8,128)(2,1)} %x_h.1, s32[1,512]{1,0:T(1,128)} %bitcast.24, f32[2,80]{1,0:T(2,128)} %bu_h.1, f32[2,80]{1,0:T(2,128)} %bv_h.1, f32[320]{0:T(512)} %ga_h.1, f32[320]{0:T(512)} %gm_h.1, ...), custom_call_target="tpu_custom_call" | custom-call | tf_op jit(solution)/shard_map/layer/pallas_call | solution.py:566
  104.1 1.6 %results.1 = (bf16[4,4,32,2560]{3,2,1,0:T(8,128)(2,1)}, bf16[160,512]{1,0:T(8,128)(2,1)}, bf16[160,512]{1,0:T(8,128)(2,1)}) custom-call(bf16[4,4,32,2560]{3,2,1,0:T(8,128)(2,1)S(1)} %get-tuple-element.9.y_v, bf16[160,512]{1,0:T(8,128)(2,1)S(1)} %get-tuple-element.10.k_v, bf16[160,512]{1,0:T(8,128)(2,1)S(1)} %get-tuple-element.11.v_v), custom_call_target="tpu_custom_call" | custom-call | tf_op jit(solution)/shard_map/results/pallas_call | solution.py:566

commit v8 on v7

--- a/solution.py
+++ b/solution.py
@@ -143,7 +143,7 @@
 
     g_g, g_k, g_v, g_o, g_u, g_d, g_r = gathers = [Gather(i, *spec) for i, spec in enumerate((
         (wg_s, 2, 1), (wk_s, HW, 80), (wv_s, 80, 48), (wo_s, 80, 48), (wu_s, SLICE, HW), (wd_s, SLICE, HW), (qp_s, CL, 16)))]
-    g_v.relay = g_o.relay = False
+    g_o.relay = False
 
     l_q.wait()
     wk_s[own] = jnp.concatenate([wqt_s[0:HW, :], wqt_s[HW:QK, :]], axis=1)
@@ -170,8 +170,9 @@
         cp.wait()
     pl.semaphore_wait(barrier, len(peers))
     g_g.start()
+    g_r.start()
     g_k.start()
-    g_r.start()
+    g_v.start()
     acc[...] = jnp.zeros_like(acc)
     u_s[...] = jnp.zeros_like(u_s)
 
@@ -195,26 +196,29 @@
     norm_cols(ME)
     pair(g_k, wk_s, qk_rows, ME)
     g_g.forward()
+    g_r.forward()
     g_k.forward()
-    g_r.forward()
-    g_v.start()
+    g_g.share()
+    g_r.share()
+    g_k.share()
+    g_v.forward()
     g_o.start()
-    g_g.share()
-    g_k.share()
-    g_r.share()
+    g_v.share()
     l_wu.wait()
     g_u.start()
     l_wd.wait()
     g_d.start()
     g_g.last()
+    g_r.last()
     for dx in (PREV, NEXT, FAR):
         norm_cols(dx)
     pair(g_k, wk_s, qk_rows, PREV)
+    pair(g_k, wk_s, qk_rows, NEXT)
     g_k.last()
-    g_r.last()
-    pair(g_k, wk_s, qk_rows, NEXT)
-    pair(g_v, wv_s, v_rows, ME)
+    for dx in (ME, PREV, NEXT):
+        pair(g_v, wv_s, v_rows, dx)
     pair(g_k, wk_s, qk_rows, FAR)
+    g_v.last()
 
     kn_s[...] = acc[HW:QK, :].astype(BF)
     l_pos.wait()
@@ -264,13 +268,8 @@
         prob = (e / jnp.sum(e, axis=0, keepdims=True)).astype(BF).astype(F32)
         sp_s[h] = jnp.sum(jnp.where(is_self, prob, 0.0), axis=0, keepdims=True)
         sc_s[h] = jnp.where(is_self, 0.0, prob)
-        if h == 0:
-            g_v.forward()
-            g_v.share()
-            g_v.last()
-
-    for dx in (PREV, NEXT, FAR):
-        pair(g_v, wv_s, v_rows, dx)
+
+    pair(g_v, wv_s, v_rows, FAR)
     vn_s[...] = acc[v_rows, :].astype(BF)
     l_v.wait()
     for h in BOTH:
@@ -285,14 +284,16 @@
 
             start = sp_s[h, :, ln] * vn_s[hr, ln].astype(F32)
             ot_s[hr, ln] = lax.fori_loop(0, CL // 8, mix, start)
-
+        if h == 0:
+            g_o.forward()
+            g_o.share()
+
+    g_o.last()
     o_s[...] = jnp.transpose(ot_s[...]).astype(BF).reshape(4, 4, 32, 160)
-    g_o.forward()
-    g_o.share()
-    g_o.last()
-    g_o.siblings()
-    for xo in range(4):
-        wof_s[:, 640 * xo:640 * xo + 640] = unpack(wo_s[2 * xo], wo_s[2 * xo + 1])
+    for dx in (ME, PREV, NEXT, FAR):
+        xo = up1(x, dx)
+        g_o.sibling(dx)
+        wof_s[:, pl.ds(pl.multiple_of(640 * xo, 128), 640)] = unpack(wo_s[2 * xo], wo_s[2 * xo + 1])
 
     place = ((z, y, zp, zm, yp, ym, yf), (y, z, yp, ym, zp, zm, zf))
 

time: 106 us -> 106 us (level)
  no operation moved by 1% of the time
where the time goes in v8:
time: 106 us
  Pallas kernels  105 us (99%)
    pallas_call x1, Pallas kernels, device_step(): call(tokens, positions.reshape(1, SEQ), bias_u, bias_v, gain_attn, gain_m...  103 us

profile of v8, /device:TPU:0, one launch (start us, length us, event | category | flops | bytes accessed | tf_op | source)
XLA Modules:
  0.0 105.5 jit_solution(15549663706896342884)
XLA Ops:
  0.6 103.1 %layer.1 = (bf16[4,4,32,2560]{3,2,1,0:T(8,128)(2,1)S(1)}, bf16[160,512]{1,0:T(8,128)(2,1)S(1)}, bf16[160,512]{1,0:T(8,128)(2,1)S(1)}) custom-call(bf16[512,2560]{1,0:T(8,128)(2,1)} %x_h.1, s32[1,512]{1,0:T(1,128)} %bitcast.24, f32[2,80]{1,0:T(2,128)} %bu_h.1, f32[2,80]{1,0:T(2,128)} %bv_h.1, f32[320]{0:T(512)} %ga_h.1, f32[320]{0:T(512)} %gm_h.1, ...), custom_call_target="tpu_custom_call" | custom-call | tf_op jit(solution)/shard_map/layer/pallas_call | solution.py:567
  103.8 1.6 %results.1 = (bf16[4,4,32,2560]{3,2,1,0:T(8,128)(2,1)}, bf16[160,512]{1,0:T(8,128)(2,1)}, bf16[160,512]{1,0:T(8,128)(2,1)}) custom-call(bf16[4,4,32,2560]{3,2,1,0:T(8,128)(2,1)S(1)} %get-tuple-element.9.y_v, bf16[160,512]{1,0:T(8,128)(2,1)S(1)} %get-tuple-element.10.k_v, bf16[160,512]{1,0:T(8,128)(2,1)S(1)} %get-tuple-element.11.v_v), custom_call_target="tpu_custom_call" | custom-call | tf_op jit(solution)/shard_map/results/pallas_call | solution.py:567

commit v9 on v8

--- a/solution.py
+++ b/solution.py
@@ -204,10 +204,6 @@
     g_v.forward()
     g_o.start()
     g_v.share()
-    l_wu.wait()
-    g_u.start()
-    l_wd.wait()
-    g_d.start()
     g_g.last()
     g_r.last()
     for dx in (PREV, NEXT, FAR):
@@ -289,6 +285,10 @@
             g_o.share()
 
     g_o.last()
+    l_wu.wait()
+    g_u.start()
+    l_wd.wait()
+    g_d.start()
     o_s[...] = jnp.transpose(ot_s[...]).astype(BF).reshape(4, 4, 32, 160)
     for dx in (ME, PREV, NEXT, FAR):
         xo = up1(x, dx)
@@ -375,7 +375,7 @@
             for hf in BOTH:
                 s2_s[ps, hf, j] = first[hf][j].total().astype(BF)
                 second[hf].put(j)
-            if j == FAR:
+            if j == NEXT:
                 between()
         own_sum = [first[hf][ME].total() for hf in BOTH]
         return [own_sum[hf] + second[hf].received() for hf in BOTH]

time: 106 us -> 105 us (level)
  no operation moved by 1% of the time
where the time goes in v9:
time: 105 us
  Pallas kernels  104 us (99%)
    pallas_call x1, Pallas kernels, device_step(): call(tokens, positions.reshape(1, SEQ), bias_u, bias_v, gain_attn, gain_m...  103 us

profile of v9, /device:TPU:0, one launch (start us, length us, event | category | flops | bytes accessed | tf_op | source)
XLA Modules:
  0.0 104.9 jit_solution(16918582607133789266)
XLA Ops:
  0.6 102.5 %layer.1 = (bf16[4,4,32,2560]{3,2,1,0:T(8,128)(2,1)S(1)}, bf16[160,512]{1,0:T(8,128)(2,1)S(1)}, bf16[160,512]{1,0:T(8,128)(2,1)S(1)}) custom-call(bf16[512,2560]{1,0:T(8,128)(2,1)} %x_h.1, s32[1,512]{1,0:T(1,128)} %bitcast.24, f32[2,80]{1,0:T(2,128)} %bu_h.1, f32[2,80]{1,0:T(2,128)} %bv_h.1, f32[320]{0:T(512)} %ga_h.1, f32[320]{0:T(512)} %gm_h.1, ...), custom_call_target="tpu_custom_call" | custom-call | tf_op jit(solution)/shard_map/layer/pallas_call | solution.py:567
  103.1 1.6 %results.1 = (bf16[4,4,32,2560]{3,2,1,0:T(8,128)(2,1)}, bf16[160,512]{1,0:T(8,128)(2,1)}, bf16[160,512]{1,0:T(8,128)(2,1)}) custom-call(bf16[4,4,32,2560]{3,2,1,0:T(8,128)(2,1)S(1)} %get-tuple-element.9.y_v, bf16[160,512]{1,0:T(8,128)(2,1)S(1)} %get-tuple-element.10.k_v, bf16[160,512]{1,0:T(8,128)(2,1)S(1)} %get-tuple-element.11.v_v), custom_call_target="tpu_custom_call" | custom-call | tf_op jit(solution)/shard_map/results/pallas_call | solution.py:567
